TPU v7x, 32 devices: a whole 2x2x4 slice. The times are simulated.
32 devices in a mesh: slab: 4 (over x, core), rep: 8 (over z, y).
Axes of the slice: x: 2, y: 2, z: 4, core: 2. Of those that a mesh axis runs over, the one named last changes fastest.
Arguments:
- image: float32 [144, 256, 256], P('slab', 'rep'), may hold values from 0.5 to 2
- sensitivity: float32 [144, 256, 256], P('slab', 'rep'), may hold values from 0.5 to 2
- system_blocks: bfloat16 [512, 128, 1024], P(('slab', 'rep')), may hold values from 0 to 0.00390625
- tile_slab: int32 [512, 1], P(('slab', 'rep')), may hold values from 0 to 3; in each aligned block of 16 rows (0 to 15, 16 to 31, ...) at most 6 rows name the same one
- tile_block: int32 [512], P(('slab', 'rep')), may hold values from 0 to 2303
- background: bfloat16 [512, 128], P(('slab', 'rep')), may hold values from 0.19921875 to 1
Outputs:
- updated: float32 [144, 256, 256], P('slab', 'rep')
Inputs may be any that keep to these rules, and one draw needn't show every extreme that they name: `tile_slab`: among the 16 tiles of one device at most 6 view the same slab, and in some devices some slab is viewed by exactly 6.
All inputs are finite; a program needn't handle non-finite values.
Results may differ from a plain program's by a relative error of at most 0.0003.
Values may be sent and summed in bfloat16 or wider, within the bound.
A program may use at most 64 MiB of HBM per device.

v0:
```python
import functools

import jax
import jax.numpy as jnp
from jax import lax
from jax.experimental import pallas as pl
from jax.experimental.pallas import tpu as pltpu
from jax.sharding import PartitionSpec as P

CAP = 6
LEVELS = 65535.0
HALF = 32768
LANES = 128
MESH = pl.DeviceIdType.MESH


def split(x, size):
    if size & (size - 1):
        return x // size, x % size
    return x >> (size.bit_length() - 1), x & (size - 1)


def exchange_kernel(
    sizes, slab_hbm, block_hbm, image_hbm, sys_hbm, bg_hbm, asked_hbm, scale_ref, back_ref,
    asked_ref, slab_v, block_v, bg_v, scale_v, image_v, blocks_v, sys_v, mine_v, slot_v, mine_s, slot_s, asked_s, send_f, recv_f, sums_v, bp_v, send_b,
    local_sem, id_sem, fetch_sem, back_sem, scale_sem,
):
    n, reps, tiles, block_rows, per_owner = sizes
    me = lax.axis_index("slab") * reps + lax.axis_index("rep")
    lane_tiles = image_v.shape[1] // LANES

    def device(d):
        return (lax.div(d, reps), lax.rem(d, reps))

    load_sys = pltpu.make_async_copy(sys_hbm, sys_v, local_sem.at[0])
    load_image = pltpu.make_async_copy(image_hbm, image_v, local_sem.at[1])
    load_slab = pltpu.make_async_copy(slab_hbm, slab_v, local_sem.at[4])
    load_block = pltpu.make_async_copy(block_hbm, block_v, local_sem.at[5])
    load_bg = pltpu.make_async_copy(bg_hbm, bg_v, local_sem.at[6])
    for load in (load_slab, load_block, load_image, load_bg, load_sys):
        load.start()

    barrier = pltpu.get_barrier_semaphore()

    def greet(i, c):
        pl.semaphore_signal(barrier, inc=1, device_id=device(lax.rem(me + i, n)), device_id_type=MESH)
        return c

    lax.fori_loop(1, n, greet, 0)

    load_slab.wait()
    load_block.wait()
    block = block_v[...]
    plane, within = split(block, per_owner * reps)
    owner, offset = split(within, per_owner)
    key = slab_v[...] * reps + owner
    value = (plane * per_owner + offset) * tiles + lax.broadcasted_iota(jnp.int32, (1, tiles), 1) + 1
    hot = key == lax.broadcasted_iota(jnp.int32, (n, tiles), 0)
    square = (tiles, tiles)
    earlier = lax.broadcasted_iota(jnp.int32, square, 0) < lax.broadcasted_iota(jnp.int32, square, 1)
    rank = jnp.dot(
        jnp.where(hot, 1.0, 0.0).astype(jnp.bfloat16),
        jnp.where(earlier, 1.0, 0.0).astype(jnp.bfloat16),
        preferred_element_type=jnp.float32,
    ).astype(jnp.int32)
    lane = lax.broadcasted_iota(jnp.int32, (n, LANES), 1)

    def tabled(row, zero):
        table = jnp.full((n, LANES), zero)
        for k in range(CAP):
            picked = jnp.sum(jnp.where(hot & (rank == k), row, zero), axis=1, keepdims=True)
            table = jnp.where(lane == k, picked, table)
        return table

    mine_v[...] = tabled(value, jnp.int32(0))
    own_rank = jnp.sum(jnp.where(hot, rank, 0), axis=0, keepdims=True)
    away = key - me
    slot = jnp.where(away < 0, away + n, away) * CAP + own_rank
    slot_v[0:1, 0:tiles] = jnp.clip(slot, 0, n * CAP - 1)
    to_slot = pltpu.make_async_copy(slot_v, slot_s, local_sem.at[2])
    to_slot.start()
    to_mine = pltpu.make_async_copy(mine_v, mine_s, local_sem.at[3])
    to_mine.start()
    asked_ref[pl.ds(0, 1), :] = mine_v[pl.ds(me, 1), :]

    pl.semaphore_wait(barrier, n - 1)

    def id_copy(i):
        d = lax.rem(me + i, n)
        return pltpu.make_async_remote_copy(
            src_ref=mine_v.at[pl.ds(d, 1)], dst_ref=asked_ref.at[pl.ds(i, 1)],
            send_sem=id_sem.at[0], recv_sem=id_sem.at[1],
            device_id=device(d), device_id_type=MESH,
        )

    def send_ids(i, c):
        id_copy(i).start()
        return c

    lax.fori_loop(1, n, send_ids, 0)
    to_slot.wait()
    to_mine.wait()
    load_image.wait()
    per_group = 8 // block_rows

    def cut(g, c):
        rows = image_v[pl.ds(pl.multiple_of(g * 8, 8), 8), :].astype(jnp.bfloat16).astype(jnp.float32)
        for u in range(per_group):
            blocks_v[g * per_group + u] = jnp.concatenate(
                [
                    rows[u * block_rows:(u + 1) * block_rows, h * LANES:(h + 1) * LANES]
                    for h in range(lane_tiles)
                ],
                axis=0,
            ).astype(jnp.bfloat16)
        return c

    lax.fori_loop(0, image_v.shape[0] // 8, cut, 0, unroll=4)
    rest = asked_ref.at[pl.ds(1, n - 1)]
    pltpu.make_async_copy(rest, rest, id_sem.at[1]).wait()
    to_asked = pltpu.make_async_copy(asked_ref, asked_s, local_sem.at[2])
    to_asked.start()
    keep_asked = pltpu.make_async_copy(asked_ref, asked_hbm, local_sem.at[3])
    keep_asked.start()
    to_asked.wait()

    def served(i, k):
        return blocks_v[split(jnp.maximum(asked_s[i, k] - 1, 0), tiles)[0]]

    for k in range(CAP):
        recv_f[k] = served(0, k)

    def far_first(j):
        return lax.rem(j, slabs) * reps + lax.rem(reps // 2 + lax.div(j, slabs), reps)

    slabs = n // reps
    own_turn = (reps - reps // 2) * slabs

    def serve(j, c):
        i = far_first(j)
        for k in range(CAP):
            send_f[i * CAP + k] = served(i, k)
        span = pl.ds(i * CAP, CAP)
        pltpu.make_async_remote_copy(
            src_ref=send_f.at[span], dst_ref=recv_f.at[span],
            send_sem=fetch_sem.at[0], recv_sem=fetch_sem.at[1],
            device_id=device(lax.rem(me + n - i, n)), device_id_type=MESH,
        ).start()
        return c

    lax.fori_loop(0, own_turn, serve, 0)
    lax.fori_loop(own_turn + 1, n, serve, 0)
    load_bg.wait()
    background = jnp.transpose(bg_v[...].astype(jnp.float32))
    load_sys.wait()
    others = recv_f.at[pl.ds(CAP, (n - 1) * CAP)]
    pltpu.make_async_copy(others, others, fetch_sem.at[1]).wait()

    forward = jnp.zeros(background.shape, jnp.float32)
    tile_lane = lax.broadcasted_iota(jnp.int32, (1, tiles), 1)
    pieces = block_rows * lane_tiles
    places = [(p % block_rows) * lane_tiles + p // block_rows for p in range(pieces)]
    for t in range(tiles):
        cells = recv_f[slot_s[0, t]].astype(jnp.float32)
        total = None
        for p, q in enumerate(places):
            term = sys_v[t, :, q * LANES:(q + 1) * LANES].astype(jnp.float32) * cells[p:p + 1, :]
            total = term if total is None else total + term
        forward = jnp.where(tile_lane == t, jnp.sum(total, axis=1, keepdims=True), forward)
    inverse = jnp.transpose(1.0 / (forward + background)).astype(jnp.bfloat16)
    tops = []
    for t in range(tiles):
        back = jnp.dot(inverse, sys_v[t], preferred_element_type=jnp.float32)
        tile = jnp.concatenate([back[t:t + 1, q * LANES:(q + 1) * LANES] for q in places], axis=0)
        sums_v[t] = tile
        tops.append(jnp.max(tile, axis=0, keepdims=True))
    peak = jnp.maximum(jnp.max(jnp.concatenate(tops, axis=0), axis=1, keepdims=True), 1e-33)
    gain = LEVELS / peak
    peaks = jnp.transpose(peak)
    for t in range(tiles):
        level = jnp.round(sums_v[t] * gain[t:t + 1, :]).astype(jnp.int32) - HALF
        bp_v[t] = jnp.clip(level, -HALF, HALF - 1).astype(jnp.int16)
    scale_v[...] = tabled(peaks * (1.0 / LEVELS), jnp.float32(0))

    def routed(d, k):
        return bp_v[split(jnp.maximum(mine_s[d, k] - 1, 0), tiles)[1]]

    for k in range(CAP):
        send_b[k] = routed(me, k)
    own_back = pltpu.make_async_copy(send_b.at[pl.ds(0, CAP)], back_ref.at[pl.ds(0, CAP)], local_sem.at[4])
    own_back.start()
    own_scale = pltpu.make_async_copy(scale_v.at[pl.ds(me, 1)], scale_ref.at[pl.ds(0, 1)], local_sem.at[5])
    own_scale.start()

    def give(j, c):
        i = far_first(j)
        d = lax.rem(me + i, n)
        for k in range(CAP):
            send_b[i * CAP + k] = routed(d, k)
        span = pl.ds(i * CAP, CAP)
        pltpu.make_async_remote_copy(
            src_ref=send_b.at[span], dst_ref=back_ref.at[span],
            send_sem=back_sem.at[0], recv_sem=back_sem.at[1],
            device_id=device(d), device_id_type=MESH,
        ).start()
        pltpu.make_async_remote_copy(
            src_ref=scale_v.at[pl.ds(d, 1)], dst_ref=scale_ref.at[pl.ds(i, 1)],
            send_sem=scale_sem.at[0], recv_sem=scale_sem.at[1],
            device_id=device(d), device_id_type=MESH,
        ).start()
        return c

    lax.fori_loop(0, own_turn, give, 0)
    lax.fori_loop(own_turn + 1, n, give, 0)
    for copy in (keep_asked, own_back, own_scale):
        copy.wait()
    scaled = scale_ref.at[pl.ds(1, n - 1)]
    pltpu.make_async_copy(scaled, scaled, scale_sem.at[0]).wait()
    pltpu.make_async_copy(scaled, scaled, scale_sem.at[1]).wait()
    pltpu.make_async_copy(mine_v.at[pl.ds(1, n - 1)], mine_v.at[pl.ds(1, n - 1)], id_sem.at[0]).wait()
    sent = send_f.at[pl.ds(CAP, (n - 1) * CAP)]
    pltpu.make_async_copy(sent, sent, fetch_sem.at[0]).wait()
    given = send_b.at[pl.ds(CAP, (n - 1) * CAP)]
    pltpu.make_async_copy(given, given, back_sem.at[0]).wait()
    landed = back_ref.at[pl.ds(CAP, (n - 1) * CAP)]
    pltpu.make_async_copy(landed, landed, back_sem.at[1]).wait()


def update_kernel(
    sizes, asked_hbm, scale_hbm, back_hbm, image_hbm, sens_hbm, out_hbm,
    asked_s, scale_s, back_ref, image_ref, sens_ref, out_ref, sums_v, in_sem, out_sem,
):
    n, tiles, block_rows = sizes
    moves = ((asked_hbm, asked_s), (scale_hbm, scale_s), (back_hbm, back_ref), (image_hbm, image_ref), (sens_hbm, sens_ref))
    loads = [pltpu.make_async_copy(src, dst, in_sem.at[j]) for j, (src, dst) in enumerate(moves)]
    for load in loads:
        load.start()
    lane_tiles = out_ref.shape[1] // LANES
    per_group = 8 // block_rows
    sums_v[...] = jnp.zeros_like(sums_v)

    def add(i, k):
        if k == CAP:
            return
        value = asked_s[i, k]

        @pl.when(value > 0)
        def _():
            level = back_ref[i * CAP + k].astype(jnp.int32) + HALF
            sums_v[split(value - 1, tiles)[0]] += level.astype(jnp.float32) * scale_s[i, k]
            add(i, k + 1)

    def one(i, c):
        add(i, 0)
        return c

    for load in loads[:3]:
        load.wait()
    lax.fori_loop(0, n, one, 0)
    for load in loads[3:]:
        load.wait()

    def finish(g, c):
        rows = pl.ds(pl.multiple_of(g * 8, 8), 8)
        sums = [sums_v[g * per_group + u] for u in range(per_group)]
        for h in range(lane_tiles):
            cols = slice(h * LANES, (h + 1) * LANES)
            total = jnp.concatenate([s[h * block_rows:(h + 1) * block_rows] for s in sums], axis=0)
            out_ref[rows, cols] = image_ref[rows, cols] * total / sens_ref[rows, cols]
        return c

    groups = out_ref.shape[0] // 8
    chunks = out_sem.shape[0]
    stores = []
    for c in range(chunks):
        first, last = groups * c // chunks, groups * (c + 1) // chunks
        lax.fori_loop(first, last, finish, 0, unroll=4)
        span = pl.ds(first * 8, (last - first) * 8)
        stores.append(pltpu.make_async_copy(out_ref.at[span], out_hbm.at[span], out_sem.at[c]))
        stores[-1].start()
    for store in stores:
        store.wait()


def local(image, sensitivity, system_blocks, tile_slab, tile_block, background):
    slabs, reps = lax.axis_size("slab"), lax.axis_size("rep")
    n = slabs * reps
    tiles, events, width = system_blocks.shape
    planes, rows, cols = image.shape
    block_rows = width // cols
    per_owner = rows // block_rows
    image2 = image.reshape(planes * rows, cols)
    sens2 = sensitivity.reshape(planes * rows, cols)
    sub = width // LANES

    hbm = pl.BlockSpec(memory_space=pltpu.HBM)
    asked, scale, back = pl.pallas_call(
        functools.partial(exchange_kernel, (n, reps, tiles, block_rows, per_owner)),
        out_shape=(
            jax.ShapeDtypeStruct((n, LANES), jnp.int32),
            jax.ShapeDtypeStruct((n, LANES), jnp.float32),
            jax.ShapeDtypeStruct((n * CAP, sub, LANES), jnp.int16),
        ),
        in_specs=[hbm] * 5,
        out_specs=(hbm, hbm, hbm),
        scratch_shapes=[
            pltpu.VMEM((n, LANES), jnp.int32),
            pltpu.VMEM((1, tiles), jnp.int32),
            pltpu.VMEM((1, tiles), jnp.int32),
            pltpu.VMEM(background.shape, jnp.bfloat16),
            pltpu.VMEM((n, LANES), jnp.float32),
            pltpu.VMEM(image2.shape, jnp.float32),
            pltpu.VMEM((planes * per_owner, sub, LANES), jnp.bfloat16),
            pltpu.VMEM(system_blocks.shape, jnp.bfloat16),
            pltpu.VMEM((n, LANES), jnp.int32),
            pltpu.VMEM((8, LANES), jnp.int32),
            pltpu.SMEM((n, LANES), jnp.int32),
            pltpu.SMEM((8, LANES), jnp.int32),
            pltpu.SMEM((n, LANES), jnp.int32),
            pltpu.VMEM((n * CAP, sub, LANES), jnp.bfloat16),
            pltpu.VMEM((n * CAP, sub, LANES), jnp.bfloat16),
            pltpu.VMEM((tiles, sub, LANES), jnp.float32),
            pltpu.VMEM((tiles, sub, LANES), jnp.int16),
            pltpu.VMEM((n * CAP, sub, LANES), jnp.int16),
            pltpu.SemaphoreType.DMA((7,)),
            pltpu.SemaphoreType.DMA((2,)),
            pltpu.SemaphoreType.DMA((2,)),
            pltpu.SemaphoreType.DMA((2,)),
            pltpu.SemaphoreType.DMA((2,)),
        ],
        compiler_params=pltpu.CompilerParams(
            collective_id=0, has_side_effects=True, vmem_limit_bytes=67043328
        ),
    )(tile_slab.reshape(1, tiles), tile_block.reshape(1, tiles), image2, system_blocks, background)
    updated = pl.pallas_call(
        functools.partial(update_kernel, (n, tiles, block_rows)),
        out_shape=jax.ShapeDtypeStruct(image2.shape, jnp.float32),
        in_specs=[hbm] * 5,
        out_specs=hbm,
        scratch_shapes=[
            pltpu.SMEM(asked.shape, jnp.int32),
            pltpu.SMEM(scale.shape, jnp.float32),
            pltpu.VMEM(back.shape, back.dtype),
            pltpu.VMEM(image2.shape, jnp.float32),
            pltpu.VMEM(image2.shape, jnp.float32),
            pltpu.VMEM(image2.shape, jnp.float32),
            pltpu.VMEM((planes * per_owner, sub, LANES), jnp.float32),
            pltpu.SemaphoreType.DMA((5,)),
            pltpu.SemaphoreType.DMA((4,)),
        ],
        compiler_params=pltpu.CompilerParams(vmem_limit_bytes=67043328),
    )(asked, scale, back, image2, sens2)
    return updated.reshape(image.shape)


def solution(mesh):
    return jax.shard_map(
        local,
        mesh=mesh,
        in_specs=(
            P("slab", "rep", None),
            P("slab", "rep", None),
            P(("slab", "rep"), None, None),
            P(("slab", "rep"), None),
            P(("slab", "rep")),
            P(("slab", "rep"), None),
        ),
        out_specs=P("slab", "rep", None),
        check_vma=False,
    )
```

profile of v0, /device:TPU:0, one launch (start us, length us, event | category | flops | bytes accessed | tf_op | source)
XLA Modules:
  0.0 37.2 jit_solution(6938483590880140734)
XLA Ops:
  0.0 34.1 %shard_map.64 = (s32[32,128]{1,0:T(8,128)}, f32[32,128]{1,0:T(8,128)}, s16[192,8,128]{2,1,0:T(8,128)(2,1)}) custom-call(s32[1,16]{1,0:T(1,128)} %bitcast.8, s32[1,16]{1,0:T(1,128)} %bitcast.9, f32[1152,256]{1,0:T(8,128)} %bitcast.5, bf16[16,128,1024]{2,1,0:T(8,128)(2,1)} %sys_hbm.1, bf16[16,128]{1,0:T(8,128)(2,1)} %bg_hbm.1), custom_call_target="tpu_custom_call" | custom-call | tf_op jit(solution)/shard_map/pallas_call | solution.py:297
  34.1 3.1 %shard_map.65 = f32[1152,256]{1,0:T(8,128)} custom-call(s32[32,128]{1,0:T(8,128)} %get-tuple-element.8.asked_hbm, f32[32,128]{1,0:T(8,128)} %get-tuple-element.9.scale_hbm, s16[192,8,128]{2,1,0:T(8,128)(2,1)} %get-tuple-element.10.back_hbm, f32[1152,256]{1,0:T(8,128)} %bitcast.6, f32[1152,256]{1,0:T(8,128)} %bitcast.7), custom_call_target="tpu_custom_call" | custom-call | tf_op jit(solution)/shard_map/pallas_call | solution.py:335
where the time goes:
time: 37.4 us; the launch traced here: 37.2 us
  Pallas kernels  37.2 us (99%)
    pallas_call x1, Pallas kernels, local(): pl.pallas_call(functools.partial(exchange_kernel, (n, reps, tiles, block_...  34.1 us
    pallas_call x1, Pallas kernels, local(): pl.pallas_call(functools.partial(update_kernel, (n, tiles, block_rows)),...  3.13 us

commit v1 on v0

--- a/solution.py
+++ b/solution.py
@@ -8,6 +8,7 @@
 from jax.sharding import PartitionSpec as P
 
 CAP = 6
+MAIN = 4
 LEVELS = 65535.0
 HALF = 32768
 LANES = 128
@@ -21,11 +22,12 @@
 
 
 def exchange_kernel(
-    sizes, slab_hbm, block_hbm, image_hbm, sys_hbm, bg_hbm, asked_hbm, scale_ref, back_ref,
+    sizes, slab_hbm, block_hbm, image_hbm, sys_hbm, bg_hbm, asked_hbm, scale_ref, back_ref, more_ref,
     asked_ref, slab_v, block_v, bg_v, scale_v, image_v, blocks_v, sys_v, mine_v, slot_v, mine_s, slot_s, asked_s, send_f, recv_f, sums_v, bp_v, send_b,
     local_sem, id_sem, fetch_sem, back_sem, scale_sem,
 ):
-    n, reps, tiles, block_rows, per_owner = sizes
+    n, reps, tiles, block_rows, per_owner, low, high = sizes
+    wide = high - low
     me = lax.axis_index("slab") * reps + lax.axis_index("rep")
     lane_tiles = image_v.shape[1] // LANES
 
@@ -67,16 +69,17 @@
 
     def tabled(row, zero):
         table = jnp.full((n, LANES), zero)
-        for k in range(CAP):
-            picked = jnp.sum(jnp.where(hot & (rank == k), row, zero), axis=1, keepdims=True)
+        for k in range(wide):
+            picked = jnp.sum(jnp.where(hot & (rank == low + k), row, zero), axis=1, keepdims=True)
             table = jnp.where(lane == k, picked, table)
         return table
 
-    mine_v[...] = tabled(value, jnp.int32(0))
     own_rank = jnp.sum(jnp.where(hot, rank, 0), axis=0, keepdims=True)
+    over = jnp.max(own_rank, axis=1, keepdims=True) // high
+    mine_v[...] = jnp.where(lane == wide, jnp.minimum(over, 1), tabled(value, jnp.int32(0)))
     away = key - me
-    slot = jnp.where(away < 0, away + n, away) * CAP + own_rank
-    slot_v[0:1, 0:tiles] = jnp.clip(slot, 0, n * CAP - 1)
+    slot = jnp.where(away < 0, away + n, away) * wide + own_rank - low
+    slot_v[0:1, 0:tiles] = jnp.clip(slot, 0, n * wide - 1)
     to_slot = pltpu.make_async_copy(slot_v, slot_s, local_sem.at[2])
     to_slot.start()
     to_mine = pltpu.make_async_copy(mine_v, mine_s, local_sem.at[3])
@@ -124,10 +127,12 @@
     keep_asked.start()
     to_asked.wait()
 
+    more_ref[0] = lax.fori_loop(0, n, lambda i, c: jnp.maximum(c, asked_s[i, wide]), jnp.int32(0), unroll=4)
+
     def served(i, k):
         return blocks_v[split(jnp.maximum(asked_s[i, k] - 1, 0), tiles)[0]]
 
-    for k in range(CAP):
+    for k in range(wide):
         recv_f[k] = served(0, k)
 
     def far_first(j):
@@ -138,9 +143,9 @@
 
     def serve(j, c):
         i = far_first(j)
-        for k in range(CAP):
-            send_f[i * CAP + k] = served(i, k)
-        span = pl.ds(i * CAP, CAP)
+        for k in range(wide):
+            send_f[i * wide + k] = served(i, k)
+        span = pl.ds(i * wide, wide)
         pltpu.make_async_remote_copy(
             src_ref=send_f.at[span], dst_ref=recv_f.at[span],
             send_sem=fetch_sem.at[0], recv_sem=fetch_sem.at[1],
@@ -153,7 +158,7 @@
     load_bg.wait()
     background = jnp.transpose(bg_v[...].astype(jnp.float32))
     load_sys.wait()
-    others = recv_f.at[pl.ds(CAP, (n - 1) * CAP)]
+    others = recv_f.at[pl.ds(wide, (n - 1) * wide)]
     pltpu.make_async_copy(others, others, fetch_sem.at[1]).wait()
 
     forward = jnp.zeros(background.shape, jnp.float32)
@@ -185,9 +190,9 @@
     def routed(d, k):
         return bp_v[split(jnp.maximum(mine_s[d, k] - 1, 0), tiles)[1]]
 
-    for k in range(CAP):
+    for k in range(wide):
         send_b[k] = routed(me, k)
-    own_back = pltpu.make_async_copy(send_b.at[pl.ds(0, CAP)], back_ref.at[pl.ds(0, CAP)], local_sem.at[4])
+    own_back = pltpu.make_async_copy(send_b.at[pl.ds(0, wide)], back_ref.at[pl.ds(0, wide)], local_sem.at[4])
     own_back.start()
     own_scale = pltpu.make_async_copy(scale_v.at[pl.ds(me, 1)], scale_ref.at[pl.ds(0, 1)], local_sem.at[5])
     own_scale.start()
@@ -195,9 +200,9 @@
     def give(j, c):
         i = far_first(j)
         d = lax.rem(me + i, n)
-        for k in range(CAP):
-            send_b[i * CAP + k] = routed(d, k)
-        span = pl.ds(i * CAP, CAP)
+        for k in range(wide):
+            send_b[i * wide + k] = routed(d, k)
+        span = pl.ds(i * wide, wide)
         pltpu.make_async_remote_copy(
             src_ref=send_b.at[span], dst_ref=back_ref.at[span],
             send_sem=back_sem.at[0], recv_sem=back_sem.at[1],
@@ -218,20 +223,24 @@
     pltpu.make_async_copy(scaled, scaled, scale_sem.at[0]).wait()
     pltpu.make_async_copy(scaled, scaled, scale_sem.at[1]).wait()
     pltpu.make_async_copy(mine_v.at[pl.ds(1, n - 1)], mine_v.at[pl.ds(1, n - 1)], id_sem.at[0]).wait()
-    sent = send_f.at[pl.ds(CAP, (n - 1) * CAP)]
+    sent = send_f.at[pl.ds(wide, (n - 1) * wide)]
     pltpu.make_async_copy(sent, sent, fetch_sem.at[0]).wait()
-    given = send_b.at[pl.ds(CAP, (n - 1) * CAP)]
+    given = send_b.at[pl.ds(wide, (n - 1) * wide)]
     pltpu.make_async_copy(given, given, back_sem.at[0]).wait()
-    landed = back_ref.at[pl.ds(CAP, (n - 1) * CAP)]
+    landed = back_ref.at[pl.ds(wide, (n - 1) * wide)]
     pltpu.make_async_copy(landed, landed, back_sem.at[1]).wait()
 
 
 def update_kernel(
-    sizes, asked_hbm, scale_hbm, back_hbm, image_hbm, sens_hbm, out_hbm,
-    asked_s, scale_s, back_ref, image_ref, sens_ref, out_ref, sums_v, in_sem, out_sem,
+    sizes, *refs,
 ):
-    n, tiles, block_rows = sizes
-    moves = ((asked_hbm, asked_s), (scale_hbm, scale_s), (back_hbm, back_ref), (image_hbm, image_ref), (sens_hbm, sens_ref))
+    n, tiles, block_rows, widths = sizes
+    parts = 3 * len(widths)
+    out_hbm = refs[parts + 2]
+    staged = refs[parts + 3:2 * parts + 5]
+    image_ref, sens_ref = staged[parts:]
+    out_ref, sums_v, in_sem, out_sem = refs[2 * parts + 5:]
+    moves = tuple(zip(refs[:parts + 2], staged))
     loads = [pltpu.make_async_copy(src, dst, in_sem.at[j]) for j, (src, dst) in enumerate(moves)]
     for load in loads:
         load.start()
@@ -239,25 +248,28 @@
     per_group = 8 // block_rows
     sums_v[...] = jnp.zeros_like(sums_v)
 
-    def add(i, k):
-        if k == CAP:
-            return
-        value = asked_s[i, k]
-
-        @pl.when(value > 0)
-        def _():
-            level = back_ref[i * CAP + k].astype(jnp.int32) + HALF
-            sums_v[split(value - 1, tiles)[0]] += level.astype(jnp.float32) * scale_s[i, k]
-            add(i, k + 1)
-
-    def one(i, c):
-        add(i, 0)
-        return c
-
-    for load in loads[:3]:
+    for load in loads[:parts]:
         load.wait()
-    lax.fori_loop(0, n, one, 0)
-    for load in loads[3:]:
+    for j, wide in enumerate(widths):
+        asked_s, scale_s, back_ref = staged[3 * j:3 * j + 3]
+
+        def add(i, k):
+            if k == wide:
+                return
+            value = asked_s[i, k]
+
+            @pl.when(value > 0)
+            def _():
+                level = back_ref[i * wide + k].astype(jnp.int32) + HALF
+                sums_v[split(value - 1, tiles)[0]] += level.astype(jnp.float32) * scale_s[i, k]
+                add(i, k + 1)
+
+        def one(i, c):
+            add(i, 0)
+            return c
+
+        lax.fori_loop(0, n, one, 0)
+    for load in loads[parts:]:
         load.wait()
 
     def finish(g, c):
@@ -294,62 +306,85 @@
     sub = width // LANES
 
     hbm = pl.BlockSpec(memory_space=pltpu.HBM)
-    asked, scale, back = pl.pallas_call(
-        functools.partial(exchange_kernel, (n, reps, tiles, block_rows, per_owner)),
-        out_shape=(
-            jax.ShapeDtypeStruct((n, LANES), jnp.int32),
-            jax.ShapeDtypeStruct((n, LANES), jnp.float32),
-            jax.ShapeDtypeStruct((n * CAP, sub, LANES), jnp.int16),
-        ),
-        in_specs=[hbm] * 5,
-        out_specs=(hbm, hbm, hbm),
-        scratch_shapes=[
-            pltpu.VMEM((n, LANES), jnp.int32),
-            pltpu.VMEM((1, tiles), jnp.int32),
-            pltpu.VMEM((1, tiles), jnp.int32),
-            pltpu.VMEM(background.shape, jnp.bfloat16),
-            pltpu.VMEM((n, LANES), jnp.float32),
-            pltpu.VMEM(image2.shape, jnp.float32),
-            pltpu.VMEM((planes * per_owner, sub, LANES), jnp.bfloat16),
-            pltpu.VMEM(system_blocks.shape, jnp.bfloat16),
-            pltpu.VMEM((n, LANES), jnp.int32),
-            pltpu.VMEM((8, LANES), jnp.int32),
-            pltpu.SMEM((n, LANES), jnp.int32),
-            pltpu.SMEM((8, LANES), jnp.int32),
-            pltpu.SMEM((n, LANES), jnp.int32),
-            pltpu.VMEM((n * CAP, sub, LANES), jnp.bfloat16),
-            pltpu.VMEM((n * CAP, sub, LANES), jnp.bfloat16),
-            pltpu.VMEM((tiles, sub, LANES), jnp.float32),
-            pltpu.VMEM((tiles, sub, LANES), jnp.int16),
-            pltpu.VMEM((n * CAP, sub, LANES), jnp.int16),
-            pltpu.SemaphoreType.DMA((7,)),
-            pltpu.SemaphoreType.DMA((2,)),
-            pltpu.SemaphoreType.DMA((2,)),
-            pltpu.SemaphoreType.DMA((2,)),
-            pltpu.SemaphoreType.DMA((2,)),
-        ],
-        compiler_params=pltpu.CompilerParams(
-            collective_id=0, has_side_effects=True, vmem_limit_bytes=67043328
-        ),
-    )(tile_slab.reshape(1, tiles), tile_block.reshape(1, tiles), image2, system_blocks, background)
-    updated = pl.pallas_call(
-        functools.partial(update_kernel, (n, tiles, block_rows)),
-        out_shape=jax.ShapeDtypeStruct(image2.shape, jnp.float32),
-        in_specs=[hbm] * 5,
-        out_specs=hbm,
-        scratch_shapes=[
-            pltpu.SMEM(asked.shape, jnp.int32),
-            pltpu.SMEM(scale.shape, jnp.float32),
-            pltpu.VMEM(back.shape, back.dtype),
-            pltpu.VMEM(image2.shape, jnp.float32),
-            pltpu.VMEM(image2.shape, jnp.float32),
-            pltpu.VMEM(image2.shape, jnp.float32),
-            pltpu.VMEM((planes * per_owner, sub, LANES), jnp.float32),
-            pltpu.SemaphoreType.DMA((5,)),
-            pltpu.SemaphoreType.DMA((4,)),
-        ],
-        compiler_params=pltpu.CompilerParams(vmem_limit_bytes=67043328),
-    )(asked, scale, back, image2, sens2)
+    scalar = pl.BlockSpec(memory_space=pltpu.SMEM)
+
+    def exchange(low, high):
+        wide = high - low
+        return pl.pallas_call(
+            functools.partial(exchange_kernel, (n, reps, tiles, block_rows, per_owner, low, high)),
+            out_shape=(
+                jax.ShapeDtypeStruct((n, LANES), jnp.int32),
+                jax.ShapeDtypeStruct((n, LANES), jnp.float32),
+                jax.ShapeDtypeStruct((n * wide, sub, LANES), jnp.int16),
+                jax.ShapeDtypeStruct((1,), jnp.int32),
+            ),
+            in_specs=[hbm] * 5,
+            out_specs=(hbm, hbm, hbm, scalar),
+            scratch_shapes=[
+                pltpu.VMEM((n, LANES), jnp.int32),
+                pltpu.VMEM((1, tiles), jnp.int32),
+                pltpu.VMEM((1, tiles), jnp.int32),
+                pltpu.VMEM(background.shape, jnp.bfloat16),
+                pltpu.VMEM((n, LANES), jnp.float32),
+                pltpu.VMEM(image2.shape, jnp.float32),
+                pltpu.VMEM((planes * per_owner, sub, LANES), jnp.bfloat16),
+                pltpu.VMEM(system_blocks.shape, jnp.bfloat16),
+                pltpu.VMEM((n, LANES), jnp.int32),
+                pltpu.VMEM((8, LANES), jnp.int32),
+                pltpu.SMEM((n, LANES), jnp.int32),
+                pltpu.SMEM((8, LANES), jnp.int32),
+                pltpu.SMEM((n, LANES), jnp.int32),
+                pltpu.VMEM((n * wide, sub, LANES), jnp.bfloat16),
+                pltpu.VMEM((n * wide, sub, LANES), jnp.bfloat16),
+                pltpu.VMEM((tiles, sub, LANES), jnp.float32),
+                pltpu.VMEM((tiles, sub, LANES), jnp.int16),
+                pltpu.VMEM((n * wide, sub, LANES), jnp.int16),
+                pltpu.SemaphoreType.DMA((7,)),
+                pltpu.SemaphoreType.DMA((2,)),
+                pltpu.SemaphoreType.DMA((2,)),
+                pltpu.SemaphoreType.DMA((2,)),
+                pltpu.SemaphoreType.DMA((2,)),
+            ],
+            compiler_params=pltpu.CompilerParams(
+                collective_id=min(low, 1), has_side_effects=True, vmem_limit_bytes=67043328
+            ),
+        )(tile_slab.reshape(1, tiles), tile_block.reshape(1, tiles), image2, system_blocks, background)
+
+    def update(*parts):
+        tables = [table for part in parts for table in part]
+        widths = tuple(part[2].shape[0] // n for part in parts)
+        staged = []
+        for asked, scale, back in parts:
+            staged += [
+                pltpu.SMEM(asked.shape, jnp.int32),
+                pltpu.SMEM(scale.shape, jnp.float32),
+                pltpu.VMEM(back.shape, back.dtype),
+            ]
+        return pl.pallas_call(
+            functools.partial(update_kernel, (n, tiles, block_rows, widths)),
+            out_shape=jax.ShapeDtypeStruct(image2.shape, jnp.float32),
+            in_specs=[hbm] * (len(tables) + 2),
+            out_specs=hbm,
+            scratch_shapes=[
+                *staged,
+                pltpu.VMEM(image2.shape, jnp.float32),
+                pltpu.VMEM(image2.shape, jnp.float32),
+                pltpu.VMEM(image2.shape, jnp.float32),
+                pltpu.VMEM((planes * per_owner, sub, LANES), jnp.float32),
+                pltpu.SemaphoreType.DMA((len(tables) + 2,)),
+                pltpu.SemaphoreType.DMA((4,)),
+            ],
+            compiler_params=pltpu.CompilerParams(vmem_limit_bytes=67043328),
+        )(*tables, image2, sens2)
+
+    *main, more = exchange(0, MAIN)
+    if MAIN == CAP:
+        return update(main).reshape(image.shape)
+    updated = lax.cond(
+        more[0] > 0,
+        lambda: update(main, exchange(MAIN, CAP)[:3]),
+        lambda: update(main),
+    )
     return updated.reshape(image.shape)
 
 

time: 37.4 us -> 33.8 us (0.904)
  Pallas kernels: 37.2 us -> 33 us
  between operations: 0.01 us -> 0.57 us
    pallas_call x2, Pallas kernels: 37.2 us -> 33 us  [the longest x1 29.9 us: exchange(): pl.pallas_call(functools.partial(exchange_kernel, (n, reps, tiles, block_...]
where the time goes in v1:
time: 33.8 us; the launch traced here: 33.6 us
  Pallas kernels  33 us (98%)
  between operations  0.57 us (2%)
    pallas_call x1, Pallas kernels, exchange(): pl.pallas_call(functools.partial(exchange_kernel, (n, reps, tiles, block_...  29.9 us
    pallas_call x1, Pallas kernels, update(): pl.pallas_call(functools.partial(update_kernel, (n, tiles, block_rows, wi...  3.14 us

profile of v1, /device:TPU:0, one launch (start us, length us, event | category | flops | bytes accessed | tf_op | source)
XLA Modules:
  0.0 33.6 jit_solution(7044310792679409403)
XLA Ops:
  0.0 29.9 %shard_map.66 = (s32[32,128]{1,0:T(8,128)}, f32[32,128]{1,0:T(8,128)}, s16[128,8,128]{2,1,0:T(8,128)(2,1)}, s32[1]{0:T(128)}) custom-call(s32[1,16]{1,0:T(1,128)} %bitcast.16, s32[1,16]{1,0:T(1,128)} %bitcast.18, f32[1152,256]{1,0:T(8,128)} %bitcast.9, bf16[16,128,1024]{2,1,0:T(8,128)(2,1)} %sys_hbm.1, bf16[16,128]{1,0:T(8,128)(2,1)} %bg_hbm.1), custom_call_target="tpu_custom_call" | custom-call | tf_op jit(solution)/shard_map/pallas_call | solution.py:313
  30.4 3.2 %conditional.1 = (f32[36,32,256]{2,1,0:T(8,128)}) conditional(s32[]{:T(128)} %bitcast.7, (s32[32,128]{1,0:T(8,128)}, f32[32,128]{1,0:T(8,128)}, s16[128,8,128]{2,1,0:T(8,128)(2,1)}, f32[1152,256]{1,0:T(8,128)}, f32[1152,256]{1,0:T(8,128)}) %tuple.21, (s32[16,1]{0,1:T(1,128)}, s32[16]{0:T(128)}, f32[1152,256]{1,0:T(8,128)}, ...), branch_computations={%region_0.0_spmd, %region_1.0_spmd} | conditional | bytes 8 | solution.py:383
  30.4 3.1 %branch_0_fun.1 = f32[1152,256]{1,0:T(8,128)} custom-call(s32[32,128]{1,0:T(8,128)} %get-tuple-element.37.refs_0_, f32[32,128]{1,0:T(8,128)} %get-tuple-element.38.refs_1_, s16[128,8,128]{2,1,0:T(8,128)(2,1)} %get-tuple-element.39.refs_2_, f32[1152,256]{1,0:T(8,128)} %get-tuple-element.40.refs_3_, f32[1152,256]{1,0:T(8,128)} %get-tuple-element.41.refs_4_), custom_call_target="tpu_custom_call" | custom-call | tf_op jit(solution)/shard_map/cond/branch_0_fun/pallas_call | solution.py:363

commit v2 on v1

v2 whole, which is shorter than its diff:
```python
import functools

import jax
import jax.numpy as jnp
from jax import lax
from jax.experimental import pallas as pl
from jax.experimental.pallas import tpu as pltpu
from jax.sharding import PartitionSpec as P

CAP = 6
MAIN = ((0, 1), (1, 4))
REST = ((4, CAP),)
LEVELS = 65535.0
HALF = 32768
LANES = 128
SUBLANES = 8
MESH = pl.DeviceIdType.MESH
VMEM_LIMIT = 32 * 1024 * 1024


def split(x, size):
    if size & (size - 1):
        return x // size, x % size
    return x >> (size.bit_length() - 1), x & (size - 1)


def listed(tiles, part):
    lo, hi = part
    return tiles if lo == 0 else tiles * (hi - lo) // hi


def padded(count):
    return -(-count // SUBLANES) * SUBLANES


def exchange_kernel(sizes, parts, *refs):
    n, reps, tiles, block_rows, per_owner = sizes
    low, high = parts[0][0], parts[-1][1]
    wide = high - low
    slab_hbm, block_hbm, image_hbm, sens_hbm, sys_hbm, bg_hbm, entry_ref, scale_ref, back_ref, ratio_ref, more_hbm = refs[:11]
    (
        more_s, asked_ref, slab_v, block_v, bg_v, scale_v, image_v, sens_v, blocks_v, sys_v, mine_v, list_v, mine_s, list_s, asked_s, sums_v,
        local_sem, id_sem, scale_sem, fetch_sem, back_sem,
    ) = refs[11:32]
    per_part = [refs[32 + 4 * c:36 + 4 * c] for c in range(len(parts))]
    me = lax.axis_index("slab") * reps + lax.axis_index("rep")
    lane_tiles = image_v.shape[1] // LANES

    def device(d):
        return (lax.div(d, reps), lax.rem(d, reps))

    def ahead_by(i):
        return lax.rem(me + i, n)

    load_sys = pltpu.make_async_copy(sys_hbm, sys_v, local_sem.at[0])
    load_image = pltpu.make_async_copy(image_hbm, image_v, local_sem.at[1])
    load_slab = pltpu.make_async_copy(slab_hbm, slab_v, local_sem.at[4])
    load_block = pltpu.make_async_copy(block_hbm, block_v, local_sem.at[5])
    load_bg = pltpu.make_async_copy(bg_hbm, bg_v, local_sem.at[6])
    load_sens = pltpu.make_async_copy(sens_hbm, sens_v, local_sem.at[4])
    for load in (load_slab, load_block, load_image, load_bg, load_sys):
        load.start()

    slabs = n // reps

    def each_partner(body):
        def line(j, carry):
            for s in range(slabs):
                body(s * reps + lax.rem(reps // 2 + j, reps))
            return carry

        far = reps - reps // 2
        lax.fori_loop(0, far, line, 0)
        for s in range(1, slabs):
            body(s * reps)
        lax.fori_loop(far + 1, reps, line, 0)

    barrier = pltpu.get_barrier_semaphore()

    def greet(i):
        pl.semaphore_signal(barrier, inc=1, device_id=device(ahead_by(i)), device_id_type=MESH)

    each_partner(greet)
    load_slab.wait()
    load_block.wait()
    load_sens.start()
    block = block_v[...]
    plane, within = split(block, per_owner * reps)
    owner, offset = split(within, per_owner)
    key = slab_v[...] * reps + owner
    tile_lane = lax.broadcasted_iota(jnp.int32, (1, tiles), 1)
    value = (plane * per_owner + offset) * tiles + 1
    hot = key == lax.broadcasted_iota(jnp.int32, (n, tiles), 0)
    square = (tiles, tiles)
    earlier = lax.broadcasted_iota(jnp.int32, square, 0) < lax.broadcasted_iota(jnp.int32, square, 1)
    earlier = jnp.where(earlier, 1.0, 0.0).astype(jnp.bfloat16)

    def before(mask):
        ones = jnp.where(mask, 1.0, 0.0).astype(jnp.bfloat16)
        return jnp.dot(ones, earlier, preferred_element_type=jnp.float32).astype(jnp.int32)

    rank = before(hot)
    lane = lax.broadcasted_iota(jnp.int32, (n, LANES), 1)

    def tabled(row, part, table):
        for k in range(*part):
            picked = jnp.sum(jnp.where(hot & (rank == k), row, jnp.zeros_like(row)), axis=1, keepdims=True)
            table = jnp.where(lane == k - low, picked, table)
        return table

    own_rank = jnp.sum(jnp.where(hot, rank, 0), axis=0, keepdims=True)
    over = jnp.max(jnp.where(own_rank >= high, 1, 0), axis=1, keepdims=True)
    table = jnp.where(lane == wide, over, 0)
    hots = []
    for c, (lo, hi) in enumerate(parts):
        slot = jnp.where(key < me, key - me + n, key - me) * (hi - lo) + own_rank - lo
        slot = jnp.clip(slot, 0, n * (hi - lo) - 1)
        row = 3 * SUBLANES * c
        if lo == 0:
            list_v[row:row + 1, 0:tiles] = slot
            hots.append(None)
            table = tabled(value + tile_lane, (lo, hi), table)
            continue
        room = padded(listed(tiles, (lo, hi)))
        mask = (own_rank >= lo) & (own_rank < hi)
        place = before(jnp.broadcast_to(mask, (room, tiles)))
        pick = (place == lax.broadcasted_iota(jnp.int32, (room, tiles), 0)) & mask
        hots.append(pick)
        tile_of = jnp.sum(jnp.where(pick, tile_lane, 0), axis=1, keepdims=True)
        slot_of = jnp.sum(jnp.where(pick, slot, 0), axis=1, keepdims=True)
        spread = lax.broadcasted_iota(jnp.int32, (room, LANES), 1)
        table = tabled(value + jnp.clip(place[0:1], 0, room - 1), (lo, hi), table)
        list_v[row + SUBLANES:row + SUBLANES + room, :] = jnp.where(spread == 0, jnp.minimum(tile_of, tiles - 1), jnp.minimum(slot_of, n * (hi - lo) - 1))
    mine_v[...] = table
    to_list = pltpu.make_async_copy(list_v, list_s, local_sem.at[2])
    to_list.start()
    to_mine = pltpu.make_async_copy(mine_v, mine_s, local_sem.at[3])
    to_mine.start()
    asked_ref[pl.ds(0, 1), :] = mine_v[pl.ds(me, 1), :]

    pl.semaphore_wait(barrier, n - 1)

    def send_ids(i):
        d = ahead_by(i)
        pltpu.make_async_remote_copy(
            src_ref=mine_v.at[pl.ds(d, 1)], dst_ref=asked_ref.at[pl.ds(i, 1)],
            send_sem=id_sem.at[0], recv_sem=id_sem.at[1],
            device_id=device(d), device_id_type=MESH,
        ).start()

    each_partner(send_ids)
    to_list.wait()
    to_mine.wait()
    load_image.wait()
    per_group = SUBLANES // block_rows

    def cut(g, c):
        rows = image_v[pl.ds(pl.multiple_of(g * SUBLANES, SUBLANES), SUBLANES), :].astype(jnp.bfloat16).astype(jnp.float32)
        for u in range(per_group):
            blocks_v[g * per_group + u] = jnp.concatenate(
                [
                    rows[u * block_rows:(u + 1) * block_rows, h * LANES:(h + 1) * LANES]
                    for h in range(lane_tiles)
                ],
                axis=0,
            ).astype(jnp.bfloat16)
        return c

    groups = image_v.shape[0] // SUBLANES
    lax.fori_loop(0, groups, cut, 0, unroll=4)
    load_sens.wait()

    def divide(g, c):
        rows = pl.ds(pl.multiple_of(g * SUBLANES, SUBLANES), SUBLANES)
        ratio_ref[rows, :] = image_v[rows, :] / sens_v[rows, :]
        return c

    lax.fori_loop(0, groups, divide, 0, unroll=4)
    load_bg.wait()
    background = bg_v[...]
    columns = []
    for pick in hots:
        if pick is None:
            columns.append(jnp.transpose(background.astype(jnp.float32)))
        else:
            ones = jnp.where(pick, 1.0, 0.0)
            chosen = jnp.dot(ones.astype(jnp.bfloat16), background, preferred_element_type=jnp.float32)
            columns.append(jnp.transpose(chosen + (1.0 - jnp.sum(ones, axis=1, keepdims=True))))
    load_sys.wait()
    rest = asked_ref.at[pl.ds(1, n - 1)]
    pltpu.make_async_copy(rest, rest, id_sem.at[1]).wait()
    to_asked = pltpu.make_async_copy(asked_ref, asked_s, local_sem.at[2])
    to_asked.start()
    to_asked.wait()

    def served(i, k):
        return blocks_v[split(jnp.maximum(asked_s[i, k] - 1, 0), tiles)[0]]

    def fetch(c):
        lo, hi = parts[c]
        span, (send_f, recv_f, _, _) = hi - lo, per_part[c]
        for k in range(span):
            recv_f[k] = served(0, lo - low + k)

        def serve(i):
            for k in range(span):
                send_f[i * span + k] = served(i, lo - low + k)
            at = pl.ds(i * span, span)
            pltpu.make_async_remote_copy(
                src_ref=send_f.at[at], dst_ref=recv_f.at[at],
                send_sem=fetch_sem.at[2 * c], recv_sem=fetch_sem.at[2 * c + 1],
                device_id=device(ahead_by(n - i)), device_id_type=MESH,
            ).start()

        each_partner(serve)

    for c in range(len(parts)):
        fetch(c)
    more_s[0] = lax.fori_loop(0, n, lambda i, m: jnp.maximum(m, asked_s[i, wide]), jnp.int32(0), unroll=4)
    keep_more = pltpu.make_async_copy(more_s, more_hbm, local_sem.at[3])
    keep_more.start()
    asked = asked_ref[...]
    below = lax.broadcasted_iota(jnp.int32, (n, n), 0) > lax.broadcasted_iota(jnp.int32, (n, n), 1)
    used = jnp.where((asked > 0) & (lane < wide), 1.0, 0.0).astype(jnp.bfloat16)
    ahead = jnp.dot(jnp.where(below, 1.0, 0.0).astype(jnp.bfloat16), used, preferred_element_type=jnp.float32).astype(jnp.int32)
    source = lax.broadcasted_iota(jnp.int32, (n, 1), 0)
    room = entry_ref.shape[1]
    position = lax.broadcasted_iota(jnp.int32, (n, room), 1)
    filled = jnp.zeros((1, 1), jnp.int32)
    entries = [jnp.zeros((1, room), jnp.int32) for _ in range(3)]
    for lo, hi in parts:
        for k in range(lo - low, hi - low):
            value_k = asked[:, k:k + 1]
            mine_k = (position == ahead[:, k:k + 1] + filled) & (value_k > 0)
            row_k = (lo - low) * n + source * (hi - lo) + k - (lo - low)
            facts = (row_k, split(value_k - 1, tiles)[0], source * wide + k)
            for f, fact in enumerate(facts):
                entries[f] += jnp.sum(jnp.where(mine_k, fact, 0), axis=0, keepdims=True)
            filled += jnp.sum(jnp.where(value_k > 0, 1, 0), axis=0, keepdims=True)
    for f, fact in enumerate(entries + [jnp.broadcast_to(filled, (1, room))]):
        entry_ref[f:f + 1, :] = fact

    pieces = block_rows * lane_tiles
    places = [(p % block_rows) * lane_tiles + p // block_rows for p in range(pieces)]
    scales = jnp.zeros((n, LANES), jnp.float32)
    for c, (lo, hi) in enumerate(parts):
        span, (send_f, recv_f, bp_v, send_b) = hi - lo, per_part[c]
        others = recv_f.at[pl.ds(span, (n - 1) * span)]
        pltpu.make_async_copy(others, others, fetch_sem.at[2 * c + 1]).wait()
        row, pick, count = 3 * SUBLANES * c, hots[c], listed(tiles, (lo, hi))
        if pick is None:
            chosen, cells_of = list(range(tiles)), [list_s[row, t] for t in range(tiles)]
        else:
            chosen = [jnp.clip(list_s[row + SUBLANES + j, 0], 0, tiles - 1) for j in range(count)]
            cells_of = [jnp.clip(list_s[row + SUBLANES + j, 1], 0, n * span - 1) for j in range(count)]
        forward = jnp.zeros(columns[c].shape, jnp.float32)
        column = lax.broadcasted_iota(jnp.int32, (1, forward.shape[1]), 1)
        for j in range(count):
            t = chosen[j]
            cells = recv_f[cells_of[j]].astype(jnp.float32)
            total = None
            for p, q in enumerate(places):
                term = sys_v[t, :, q * LANES:(q + 1) * LANES].astype(jnp.float32) * cells[p:p + 1, :]
                total = term if total is None else total + term
            forward = jnp.where(column == j, jnp.sum(total, axis=1, keepdims=True), forward)
        inverse = jnp.transpose(1.0 / (forward + columns[c])).astype(jnp.bfloat16)
        tops = []
        for j in range(count):
            back = jnp.dot(inverse, sys_v[chosen[j]], preferred_element_type=jnp.float32)
            tile = jnp.concatenate([back[j:j + 1, q * LANES:(q + 1) * LANES] for q in places], axis=0)
            sums_v[j] = tile
            tops.append(jnp.max(tile, axis=0, keepdims=True))
        peak = jnp.maximum(jnp.max(jnp.concatenate(tops, axis=0), axis=1, keepdims=True), 1e-33)
        gain = LEVELS / peak
        for j in range(count):
            level = jnp.round(sums_v[j] * gain[j:j + 1, :]).astype(jnp.int32) - HALF
            bp_v[j] = jnp.clip(level, -HALF, HALF - 1).astype(jnp.int16)

        def routed(d, k):
            return bp_v[split(jnp.maximum(mine_s[d, lo - low + k] - 1, 0), tiles)[1]]

        def give(i):
            d = ahead_by(i)
            for k in range(span):
                send_b[i * span + k] = routed(d, k)
            pltpu.make_async_remote_copy(
                src_ref=send_b.at[pl.ds(i * span, span)], dst_ref=back_ref.at[pl.ds((lo - low) * n + i * span, span)],
                send_sem=back_sem.at[2 * c], recv_sem=back_sem.at[2 * c + 1],
                device_id=device(d), device_id_type=MESH,
            ).start()

        each_partner(give)
        for k in range(span):
            back_ref[(lo - low) * n + k] = routed(me, k)
        if pick is None:
            peaks = jnp.transpose(peak)
        else:
            peaks = jnp.sum(jnp.where(pick[:count], peak, 0.0), axis=0, keepdims=True)
        scales = tabled(peaks * (1.0 / LEVELS), (lo, hi), scales)

    scale_v[...] = scales
    scale_ref[pl.ds(0, 1), :] = scale_v[pl.ds(me, 1), :]

    def give_scale(i):
        d = ahead_by(i)
        pltpu.make_async_remote_copy(
            src_ref=scale_v.at[pl.ds(d, 1)], dst_ref=scale_ref.at[pl.ds(i, 1)],
            send_sem=scale_sem.at[0], recv_sem=scale_sem.at[1],
            device_id=device(d), device_id_type=MESH,
        ).start()

    each_partner(give_scale)
    keep_more.wait()
    scaled = scale_ref.at[pl.ds(1, n - 1)]
    pltpu.make_async_copy(scaled, scaled, scale_sem.at[0]).wait()
    pltpu.make_async_copy(rest, rest, id_sem.at[0]).wait()
    for c, (lo, hi) in enumerate(parts):
        span, (send_f, recv_f, bp_v, send_b) = hi - lo, per_part[c]
        sent = send_f.at[pl.ds(span, (n - 1) * span)]
        pltpu.make_async_copy(sent, sent, fetch_sem.at[2 * c]).wait()
        given = send_b.at[pl.ds(span, (n - 1) * span)]
        pltpu.make_async_copy(given, given, back_sem.at[2 * c]).wait()
        landed = back_ref.at[pl.ds((lo - low) * n + span, (n - 1) * span)]
        pltpu.make_async_copy(landed, landed, back_sem.at[2 * c + 1]).wait()
    pltpu.make_async_copy(scaled, scaled, scale_sem.at[1]).wait()


def update_kernel(sizes, widths, *refs):
    block_rows, = sizes
    tables = 3 * len(widths)
    ratio_ref, out_hbm = refs[tables:tables + 2]
    out_ref, in_sem, out_sem = refs[-3:]
    smem = refs[tables + 2:-3]
    loads = []
    for j in range(len(widths)):
        loads += [
            pltpu.make_async_copy(refs[3 * j], smem[2 * j], in_sem.at[2 * j]),
            pltpu.make_async_copy(refs[3 * j + 1], smem[2 * j + 1], in_sem.at[2 * j + 1]),
        ]
    for load in loads:
        load.start()
    lane_tiles = out_ref.shape[1] // LANES
    per_group = SUBLANES // block_rows
    groups = out_ref.shape[0] // SUBLANES

    def clear(g, c):
        out_ref[pl.ds(pl.multiple_of(g * SUBLANES, SUBLANES), SUBLANES), :] = jnp.zeros((SUBLANES, out_ref.shape[1]), jnp.float32)
        return c

    lax.fori_loop(0, groups, clear, 0, unroll=8)
    for load in loads:
        load.wait()
    part_of_row = split(lax.broadcasted_iota(jnp.int32, (SUBLANES, LANES), 0), block_rows)[0]
    for j, wide in enumerate(widths):
        entry_s, scale_s, back_ref = smem[2 * j], smem[2 * j + 1], refs[3 * j + 2]

        def one(e, c):
            row, block, source = entry_s[0, e], entry_s[1, e], entry_s[2, e]
            i, k = split(source, wide)
            g, part = split(block, per_group)
            level = (back_ref[row].astype(jnp.int32) + HALF).astype(jnp.float32) * scale_s[i, k]
            rows = pl.ds(pl.multiple_of(g * SUBLANES, SUBLANES), SUBLANES)
            for h in range(lane_tiles):
                cols = slice(h * LANES, (h + 1) * LANES)
                piece = jnp.concatenate([level[h * block_rows:(h + 1) * block_rows]] * per_group, axis=0)
                out_ref[rows, cols] += jnp.where(part_of_row == part, piece * ratio_ref[rows, cols], 0.0)
            return c

        lax.fori_loop(0, entry_s[3, 0], one, 0)
    store = pltpu.make_async_copy(out_ref, out_hbm, out_sem)
    store.start()
    store.wait()


def local(image, sensitivity, system_blocks, tile_slab, tile_block, background):
    slabs, reps = lax.axis_size("slab"), lax.axis_size("rep")
    n = slabs * reps
    tiles, events, width = system_blocks.shape
    planes, rows, cols = image.shape
    block_rows = width // cols
    per_owner = rows // block_rows
    image2 = image.reshape(planes * rows, cols)
    sens2 = sensitivity.reshape(planes * rows, cols)
    sub = width // LANES
    blocks = planes * per_owner

    hbm = pl.BlockSpec(memory_space=pltpu.HBM)
    vmem = pl.BlockSpec(memory_space=pltpu.VMEM)

    def exchange(parts, collective_id):
        wide = parts[-1][1] - parts[0][0]
        rows_of_lists = 3 * SUBLANES * len(parts)
        buffers = []
        for lo, hi in parts:
            room = n * (hi - lo)
            buffers += [
                pltpu.VMEM((room, sub, LANES), jnp.bfloat16),
                pltpu.VMEM((room, sub, LANES), jnp.bfloat16),
                pltpu.VMEM((tiles, sub, LANES), jnp.int16),
                pltpu.VMEM((room, sub, LANES), jnp.int16),
            ]
        return pl.pallas_call(
            functools.partial(exchange_kernel, (n, reps, tiles, block_rows, per_owner), parts),
            out_shape=(
                pltpu.VMEM((SUBLANES, -(-n * wide // LANES) * LANES), jnp.int32),
                pltpu.VMEM((n, LANES), jnp.float32),
                pltpu.VMEM((n * wide, sub, LANES), jnp.int16),
                pltpu.VMEM(image2.shape, jnp.float32),
                pltpu.HBM((LANES,), jnp.int32),
            ),
            in_specs=[hbm] * 6,
            out_specs=(vmem, vmem, vmem, vmem, hbm),
            scratch_shapes=[
                pltpu.SMEM((LANES,), jnp.int32),
                pltpu.VMEM((n, LANES), jnp.int32),
                pltpu.VMEM((1, tiles), jnp.int32),
                pltpu.VMEM((1, tiles), jnp.int32),
                pltpu.VMEM(background.shape, jnp.bfloat16),
                pltpu.VMEM((n, LANES), jnp.float32),
                pltpu.VMEM(image2.shape, jnp.float32),
                pltpu.VMEM(image2.shape, jnp.float32),
                pltpu.VMEM((blocks, sub, LANES), jnp.bfloat16),
                pltpu.VMEM(system_blocks.shape, jnp.bfloat16),
                pltpu.VMEM((n, LANES), jnp.int32),
                pltpu.VMEM((rows_of_lists, LANES), jnp.int32),
                pltpu.SMEM((n, LANES), jnp.int32),
                pltpu.SMEM((rows_of_lists, LANES), jnp.int32),
                pltpu.SMEM((n, LANES), jnp.int32),
                pltpu.VMEM((tiles, sub, LANES), jnp.float32),
                pltpu.SemaphoreType.DMA((7,)),
                pltpu.SemaphoreType.DMA((2,)),
                pltpu.SemaphoreType.DMA((2,)),
                pltpu.SemaphoreType.DMA((2 * len(parts),)),
                pltpu.SemaphoreType.DMA((2 * len(parts),)),
                *buffers,
            ],
            compiler_params=pltpu.CompilerParams(
                collective_id=collective_id, has_side_effects=True, vmem_limit_bytes=VMEM_LIMIT
            ),
        )(tile_slab.reshape(1, tiles), tile_block.reshape(1, tiles), image2, sens2, system_blocks, background)

    def update(*results):
        tables = [table for result in results for table in result[:3]]
        widths = tuple(result[2].shape[0] // n for result in results)
        staged = []
        for entries, scale, _ in (result[:3] for result in results):
            staged += [pltpu.SMEM(entries.shape, jnp.int32), pltpu.SMEM(scale.shape, jnp.float32)]
        return pl.pallas_call(
            functools.partial(update_kernel, (block_rows,), widths),
            out_shape=pltpu.HBM(image2.shape, jnp.float32),
            in_specs=[vmem] * (len(tables) + 1),
            out_specs=hbm,
            scratch_shapes=[
                *staged,
                pltpu.VMEM(image2.shape, jnp.float32),
                pltpu.SemaphoreType.DMA((len(staged),)),
                pltpu.SemaphoreType.DMA,
            ],
            compiler_params=pltpu.CompilerParams(vmem_limit_bytes=VMEM_LIMIT),
        )(*tables, results[0][3])

    main = exchange(MAIN, 0)
    updated = lax.cond(
        main[4][0] > 0,
        lambda: update(main, exchange(REST, 1)),
        lambda: update(main),
    )
    return updated.reshape(image.shape)


def solution(mesh):
    return jax.shard_map(
        local,
        mesh=mesh,
        in_specs=(
            P("slab", "rep", None),
            P("slab", "rep", None),
            P(("slab", "rep"), None, None),
            P(("slab", "rep"), None),
            P(("slab", "rep")),
            P(("slab", "rep"), None),
        ),
        out_specs=P("slab", "rep", None),
        check_vma=False,
    )
```

time: 33.8 us -> 31.3 us (0.926)
  Pallas kernels: 33 us -> 30.4 us
    pallas_call x1, Pallas kernels: 29.9 us -> 28.1 us  [exchange(): pl.pallas_call(functools.partial(exchange_kernel, (n, reps, tiles, block_...]
    pallas_call x1, Pallas kernels: 3.14 us -> 2.32 us  [update(): pl.pallas_call(functools.partial(update_kernel, (block_rows,), widths), o...]
where the time goes in v2:
time: 31.3 us; the launch traced here: 31.2 us
  Pallas kernels  30.4 us (97%)
  between operations  0.7 us (2%)
    pallas_call x1, Pallas kernels, exchange(): pl.pallas_call(functools.partial(exchange_kernel, (n, reps, tiles, block_...  28.1 us
    pallas_call x1, Pallas kernels, update(): pl.pallas_call(functools.partial(update_kernel, (block_rows,), widths), o...  2.32 us

profile of v2, /device:TPU:0, one launch (start us, length us, event | category | flops | bytes accessed | tf_op | source)
XLA Modules:
  0.0 31.2 jit_solution(11174436407663600882)
XLA Ops:
  0.0 0.0 copy-start
  0.0 0.0 copy-start.1
  0.0 0.0 copy-start.2
  0.0 0.0 copy-start.3
  0.0 0.0 copy-start.4
  0.0 0.0 copy-start.5
  0.0 28.1 %shard_map.66 = (s32[8,128]{1,0:T(8,128)S(1)}, f32[32,128]{1,0:T(8,128)S(1)}, s16[128,8,128]{2,1,0:T(8,128)(2,1)S(1)}, f32[1152,256]{1,0:T(8,128)S(1)}, s32[128]{0:T(128)}) custom-call(s32[1,16]{1,0:T(1,128)} %bitcast.16, s32[1,16]{1,0:T(1,128)} %bitcast.18, f32[1152,256]{1,0:T(8,128)} %bitcast.10, f32[1152,256]{1,0:T(8,128)} %bitcast.12, ...), custom_call_target="tpu_custom_call" | custom-call | tf_op jit(solution)/shard_map/pallas_call | solution.py:402
  28.8 0.0 copy-done
  28.8 0.0 copy-done.1
  28.8 0.0 copy-done.2
  28.8 0.0 copy-done.3
  28.8 0.0 copy-done.4
  28.8 0.0 copy-done.5
  28.9 2.3 %conditional.1 = (f32[36,32,256]{2,1,0:T(8,128)}) conditional(s32[]{:T(128)} %bitcast.8, (s32[8,128]{1,0:T(8,128)S(1)}, f32[32,128]{1,0:T(8,128)S(1)}, s16[128,8,128]{2,1,0:T(8,128)(2,1)S(1)}, f32[1152,256]{1,0:T(8,128)S(1)}) %tuple.13, (s32[16,1]{0,1:T(1,128)S(1)}, s32[16]{0:T(128)S(1)}, f32[1152,256]{1,0:T(8,128)S(1)}, f32[1152,256]{1,0:T(8,128)S(1)}, ...), branch_computations={%region_0.0_spmd, %region_1.0_spmd} | conditional | bytes 8 | solution.py:463
  28.9 2.3 %branch_0_fun.1 = f32[1152,256]{1,0:T(8,128)} custom-call(s32[8,128]{1,0:T(8,128)S(1)} %get-tuple-element.37.refs_0_, f32[32,128]{1,0:T(8,128)S(1)} %get-tuple-element.38.refs_1_, s16[128,8,128]{2,1,0:T(8,128)(2,1)S(1)} %get-tuple-element.39.refs_2_, f32[1152,256]{1,0:T(8,128)S(1)} %get-tuple-element.40.refs_3_), custom_call_target="tpu_custom_call" | custom-call | tf_op jit(solution)/shard_map/cond/branch_0_fun/pallas_call | solution.py:448
Async XLA Ops:
  0.0 28.8 %copy-start = (bf16[16,128,1024]{2,1,0:T(8,128)(2,1)S(1)}, bf16[16,128,1024]{2,1,0:T(8,128)(2,1)}, u32[]{:S(2)}) copy-start(bf16[16,128,1024]{2,1,0:T(8,128)(2,1)} %refs_4_.1) | copy-start | bytes 12582916
  0.0 28.8 %copy-start.1 = (f32[36,32,256]{2,1,0:T(8,128)S(1)}, f32[36,32,256]{2,1,0:T(8,128)}, u32[]{:S(2)}) copy-start(f32[36,32,256]{2,1,0:T(8,128)} %param.8) | copy-start | bytes 3538948
  0.0 28.8 %copy-start.2 = (f32[36,32,256]{2,1,0:T(8,128)S(1)}, f32[36,32,256]{2,1,0:T(8,128)}, u32[]{:S(2)}) copy-start(f32[36,32,256]{2,1,0:T(8,128)} %param.9) | copy-start | bytes 3538948
  0.0 28.8 %copy-start.3 = (bf16[16,128]{1,0:T(8,128)(2,1)S(1)}, bf16[16,128]{1,0:T(8,128)(2,1)}, u32[]{:S(2)}) copy-start(bf16[16,128]{1,0:T(8,128)(2,1)} %refs_5_.1) | copy-start | bytes 12292
  0.0 28.8 %copy-start.4 = (s32[16,1]{0,1:T(1,128)S(1)}, s32[16,1]{0,1:T(1,128)}, u32[]{:S(2)}) copy-start(s32[16,1]{0,1:T(1,128)} %param.11) | copy-start | bytes 196
  0.0 28.8 %copy-start.5 = (s32[16]{0:T(128)S(1)}, s32[16]{0:T(128)}, u32[]{:S(2)}) copy-start(s32[16]{0:T(128)} %param.12) | copy-start | bytes 196

commit v3 on v2

--- a/solution.py
+++ b/solution.py
@@ -37,9 +37,9 @@
     n, reps, tiles, block_rows, per_owner = sizes
     low, high = parts[0][0], parts[-1][1]
     wide = high - low
-    slab_hbm, block_hbm, image_hbm, sens_hbm, sys_hbm, bg_hbm, entry_ref, scale_ref, back_ref, ratio_ref, more_hbm = refs[:11]
+    slab_hbm, block_hbm, image_hbm, sens_hbm, sys_hbm, bg_hbm, entry_ref, scale_ref, back_ref, ratio_ref, more_ref = refs[:11]
     (
-        more_s, asked_ref, slab_v, block_v, bg_v, scale_v, image_v, sens_v, blocks_v, sys_v, mine_v, list_v, mine_s, list_s, asked_s, sums_v,
+        turned_v, asked_ref, slab_v, block_v, bg_v, scale_v, image_v, sens_v, blocks_v, sys_v, mine_v, list_v, mine_s, list_s, asked_s, sums_v,
         local_sem, id_sem, scale_sem, fetch_sem, back_sem,
     ) = refs[11:32]
     per_part = [refs[32 + 4 * c:36 + 4 * c] for c in range(len(parts))]
@@ -47,10 +47,7 @@
     lane_tiles = image_v.shape[1] // LANES
 
     def device(d):
-        return (lax.div(d, reps), lax.rem(d, reps))
-
-    def ahead_by(i):
-        return lax.rem(me + i, n)
+        return split(d, reps)
 
     load_sys = pltpu.make_async_copy(sys_hbm, sys_v, local_sem.at[0])
     load_image = pltpu.make_async_copy(image_hbm, image_v, local_sem.at[1])
@@ -66,19 +63,17 @@
     def each_partner(body):
         def line(j, carry):
             for s in range(slabs):
-                body(s * reps + lax.rem(reps // 2 + j, reps))
+                body((slabs - 1 - s) * reps + reps - 1 - j)
             return carry
 
-        far = reps - reps // 2
-        lax.fori_loop(0, far, line, 0)
-        for s in range(1, slabs):
-            body(s * reps)
-        lax.fori_loop(far + 1, reps, line, 0)
+        lax.fori_loop(0, reps - 1, line, 0)
+        for s in range(slabs - 1):
+            body((slabs - 1 - s) * reps)
 
     barrier = pltpu.get_barrier_semaphore()
 
     def greet(i):
-        pl.semaphore_signal(barrier, inc=1, device_id=device(ahead_by(i)), device_id_type=MESH)
+        pl.semaphore_signal(barrier, inc=1, device_id=device(me ^ i), device_id_type=MESH)
 
     each_partner(greet)
     load_slab.wait()
@@ -113,7 +108,7 @@
     table = jnp.where(lane == wide, over, 0)
     hots = []
     for c, (lo, hi) in enumerate(parts):
-        slot = jnp.where(key < me, key - me + n, key - me) * (hi - lo) + own_rank - lo
+        slot = (key ^ me) * (hi - lo) + own_rank - lo
         slot = jnp.clip(slot, 0, n * (hi - lo) - 1)
         row = 3 * SUBLANES * c
         if lo == 0:
@@ -130,7 +125,7 @@
         slot_of = jnp.sum(jnp.where(pick, slot, 0), axis=1, keepdims=True)
         spread = lax.broadcasted_iota(jnp.int32, (room, LANES), 1)
         table = tabled(value + jnp.clip(place[0:1], 0, room - 1), (lo, hi), table)
-        list_v[row + SUBLANES:row + SUBLANES + room, :] = jnp.where(spread == 0, jnp.minimum(tile_of, tiles - 1), jnp.minimum(slot_of, n * (hi - lo) - 1))
+        list_v[row + SUBLANES:row + SUBLANES + room, :] = jnp.where(spread == 0, tile_of, slot_of)
     mine_v[...] = table
     to_list = pltpu.make_async_copy(list_v, list_s, local_sem.at[2])
     to_list.start()
@@ -141,7 +136,7 @@
     pl.semaphore_wait(barrier, n - 1)
 
     def send_ids(i):
-        d = ahead_by(i)
+        d = me ^ i
         pltpu.make_async_remote_copy(
             src_ref=mine_v.at[pl.ds(d, 1)], dst_ref=asked_ref.at[pl.ds(i, 1)],
             send_sem=id_sem.at[0], recv_sem=id_sem.at[1],
@@ -189,12 +184,13 @@
     load_sys.wait()
     rest = asked_ref.at[pl.ds(1, n - 1)]
     pltpu.make_async_copy(rest, rest, id_sem.at[1]).wait()
-    to_asked = pltpu.make_async_copy(asked_ref, asked_s, local_sem.at[2])
+    turned_v[:, 0:n] = jnp.transpose(asked_ref[...])[0:SUBLANES]
+    to_asked = pltpu.make_async_copy(turned_v, asked_s, local_sem.at[2])
     to_asked.start()
     to_asked.wait()
 
     def served(i, k):
-        return blocks_v[split(jnp.maximum(asked_s[i, k] - 1, 0), tiles)[0]]
+        return blocks_v[split(jnp.maximum(asked_s[k, i] - 1, 0), tiles)[0]]
 
     def fetch(c):
         lo, hi = parts[c]
@@ -209,17 +205,16 @@
             pltpu.make_async_remote_copy(
                 src_ref=send_f.at[at], dst_ref=recv_f.at[at],
                 send_sem=fetch_sem.at[2 * c], recv_sem=fetch_sem.at[2 * c + 1],
-                device_id=device(ahead_by(n - i)), device_id_type=MESH,
+                device_id=device(me ^ i), device_id_type=MESH,
             ).start()
 
         each_partner(serve)
 
     for c in range(len(parts)):
         fetch(c)
-    more_s[0] = lax.fori_loop(0, n, lambda i, m: jnp.maximum(m, asked_s[i, wide]), jnp.int32(0), unroll=4)
-    keep_more = pltpu.make_async_copy(more_s, more_hbm, local_sem.at[3])
-    keep_more.start()
     asked = asked_ref[...]
+    flagged = jnp.max(jnp.where(lane == wide, asked, 0), axis=0, keepdims=True)
+    more_ref[...] = jnp.broadcast_to(jnp.max(flagged, axis=1, keepdims=True), (1, LANES))
     below = lax.broadcasted_iota(jnp.int32, (n, n), 0) > lax.broadcasted_iota(jnp.int32, (n, n), 1)
     used = jnp.where((asked > 0) & (lane < wide), 1.0, 0.0).astype(jnp.bfloat16)
     ahead = jnp.dot(jnp.where(below, 1.0, 0.0).astype(jnp.bfloat16), used, preferred_element_type=jnp.float32).astype(jnp.int32)
@@ -280,7 +275,7 @@
             return bp_v[split(jnp.maximum(mine_s[d, lo - low + k] - 1, 0), tiles)[1]]
 
         def give(i):
-            d = ahead_by(i)
+            d = me ^ i
             for k in range(span):
                 send_b[i * span + k] = routed(d, k)
             pltpu.make_async_remote_copy(
@@ -302,7 +297,7 @@
     scale_ref[pl.ds(0, 1), :] = scale_v[pl.ds(me, 1), :]
 
     def give_scale(i):
-        d = ahead_by(i)
+        d = me ^ i
         pltpu.make_async_remote_copy(
             src_ref=scale_v.at[pl.ds(d, 1)], dst_ref=scale_ref.at[pl.ds(i, 1)],
             send_sem=scale_sem.at[0], recv_sem=scale_sem.at[1],
@@ -310,7 +305,6 @@
         ).start()
 
     each_partner(give_scale)
-    keep_more.wait()
     scaled = scale_ref.at[pl.ds(1, n - 1)]
     pltpu.make_async_copy(scaled, scaled, scale_sem.at[0]).wait()
     pltpu.make_async_copy(rest, rest, id_sem.at[0]).wait()
@@ -330,15 +324,16 @@
     tables = 3 * len(widths)
     ratio_ref, out_hbm = refs[tables:tables + 2]
     out_ref, in_sem, out_sem = refs[-3:]
-    smem = refs[tables + 2:-3]
+    staged = refs[tables + 2:-3]
     loads = []
     for j in range(len(widths)):
-        loads += [
-            pltpu.make_async_copy(refs[3 * j], smem[2 * j], in_sem.at[2 * j]),
-            pltpu.make_async_copy(refs[3 * j + 1], smem[2 * j + 1], in_sem.at[2 * j + 1]),
-        ]
-    for load in loads:
-        load.start()
+        entry_s, scale_s, turned_v = staged[3 * j:3 * j + 3]
+        loads.append(pltpu.make_async_copy(refs[3 * j], entry_s, in_sem.at[2 * j]))
+        loads[-1].start()
+        scale_ref = refs[3 * j + 1]
+        turned_v[:, 0:scale_ref.shape[0]] = jnp.transpose(scale_ref[...])[0:SUBLANES]
+        loads.append(pltpu.make_async_copy(turned_v, scale_s, in_sem.at[2 * j + 1]))
+        loads[-1].start()
     lane_tiles = out_ref.shape[1] // LANES
     per_group = SUBLANES // block_rows
     groups = out_ref.shape[0] // SUBLANES
@@ -352,13 +347,13 @@
         load.wait()
     part_of_row = split(lax.broadcasted_iota(jnp.int32, (SUBLANES, LANES), 0), block_rows)[0]
     for j, wide in enumerate(widths):
-        entry_s, scale_s, back_ref = smem[2 * j], smem[2 * j + 1], refs[3 * j + 2]
+        entry_s, scale_s, back_ref = staged[3 * j], staged[3 * j + 1], refs[3 * j + 2]
 
         def one(e, c):
             row, block, source = entry_s[0, e], entry_s[1, e], entry_s[2, e]
             i, k = split(source, wide)
             g, part = split(block, per_group)
-            level = (back_ref[row].astype(jnp.int32) + HALF).astype(jnp.float32) * scale_s[i, k]
+            level = (back_ref[row].astype(jnp.int32) + HALF).astype(jnp.float32) * scale_s[k, i]
             rows = pl.ds(pl.multiple_of(g * SUBLANES, SUBLANES), SUBLANES)
             for h in range(lane_tiles):
                 cols = slice(h * LANES, (h + 1) * LANES)
@@ -406,12 +401,12 @@
                 pltpu.VMEM((n, LANES), jnp.float32),
                 pltpu.VMEM((n * wide, sub, LANES), jnp.int16),
                 pltpu.VMEM(image2.shape, jnp.float32),
-                pltpu.HBM((LANES,), jnp.int32),
+                pltpu.VMEM((1, LANES), jnp.int32),
             ),
             in_specs=[hbm] * 6,
-            out_specs=(vmem, vmem, vmem, vmem, hbm),
+            out_specs=(vmem,) * 5,
             scratch_shapes=[
-                pltpu.SMEM((LANES,), jnp.int32),
+                pltpu.VMEM((SUBLANES, max(n, LANES)), jnp.int32),
                 pltpu.VMEM((n, LANES), jnp.int32),
                 pltpu.VMEM((1, tiles), jnp.int32),
                 pltpu.VMEM((1, tiles), jnp.int32),
@@ -425,7 +420,7 @@
                 pltpu.VMEM((rows_of_lists, LANES), jnp.int32),
                 pltpu.SMEM((n, LANES), jnp.int32),
                 pltpu.SMEM((rows_of_lists, LANES), jnp.int32),
-                pltpu.SMEM((n, LANES), jnp.int32),
+                pltpu.SMEM((SUBLANES, max(n, LANES)), jnp.int32),
                 pltpu.VMEM((tiles, sub, LANES), jnp.float32),
                 pltpu.SemaphoreType.DMA((7,)),
                 pltpu.SemaphoreType.DMA((2,)),
@@ -443,8 +438,13 @@
         tables = [table for result in results for table in result[:3]]
         widths = tuple(result[2].shape[0] // n for result in results)
         staged = []
-        for entries, scale, _ in (result[:3] for result in results):
-            staged += [pltpu.SMEM(entries.shape, jnp.int32), pltpu.SMEM(scale.shape, jnp.float32)]
+        for entries, _, _ in (result[:3] for result in results):
+            turned = (SUBLANES, max(n, LANES))
+            staged += [
+                pltpu.SMEM(entries.shape, jnp.int32),
+                pltpu.SMEM(turned, jnp.float32),
+                pltpu.VMEM(turned, jnp.float32),
+            ]
         return pl.pallas_call(
             functools.partial(update_kernel, (block_rows,), widths),
             out_shape=pltpu.HBM(image2.shape, jnp.float32),
@@ -453,7 +453,7 @@
             scratch_shapes=[
                 *staged,
                 pltpu.VMEM(image2.shape, jnp.float32),
-                pltpu.SemaphoreType.DMA((len(staged),)),
+                pltpu.SemaphoreType.DMA((2 * len(results),)),
                 pltpu.SemaphoreType.DMA,
             ],
             compiler_params=pltpu.CompilerParams(vmem_limit_bytes=VMEM_LIMIT),
@@ -461,7 +461,7 @@
 
     main = exchange(MAIN, 0)
     updated = lax.cond(
-        main[4][0] > 0,
+        main[4][0, 0] > 0,
         lambda: update(main, exchange(REST, 1)),
         lambda: update(main),
     )

time: 31.3 us -> 29.8 us (0.952)
  Pallas kernels: 30.4 us -> 29.7 us
  between operations: 0.7 us -> 0.11 us
    pallas_call x1, Pallas kernels: 28.1 us -> 27.6 us  [exchange(): pl.pallas_call(functools.partial(exchange_kernel, (n, reps, tiles, block_...]
where the time goes in v3:
time: 29.8 us; the launch traced here: 29.9 us
  Pallas kernels  29.7 us (100%)
    pallas_call x1, Pallas kernels, exchange(): pl.pallas_call(functools.partial(exchange_kernel, (n, reps, tiles, block_...  27.6 us
    pallas_call x1, Pallas kernels, update(): pl.pallas_call(functools.partial(update_kernel, (block_rows,), widths), o...  2.11 us

profile of v3, /device:TPU:0, one launch (start us, length us, event | category | flops | bytes accessed | tf_op | source)
XLA Modules:
  0.0 29.9 jit_solution(339554827504360491)
XLA Ops:
  0.0 0.0 copy-start
  0.0 0.0 copy-start.1
  0.0 0.0 copy-start.2
  0.0 0.0 copy-start.3
  0.0 0.0 copy-start.4
  0.0 0.0 copy-start.5
  0.0 27.6 %shard_map.66 = (s32[8,128]{1,0:T(8,128)S(1)}, f32[32,128]{1,0:T(8,128)S(1)}, s16[128,8,128]{2,1,0:T(8,128)(2,1)S(1)}, f32[1152,256]{1,0:T(8,128)S(1)}, s32[1,128]{1,0:T(1,128)S(1)}) custom-call(s32[1,16]{1,0:T(1,128)} %bitcast.17, s32[1,16]{1,0:T(1,128)} %bitcast.19, f32[1152,256]{1,0:T(8,128)} %bitcast.11, f32[1152,256]{1,0:T(8,128)} %bitcast.13, ...), custom_call_target="tpu_custom_call" | custom-call | tf_op jit(solution)/shard_map/pallas_call | solution.py:397
  27.7 0.0 copy-done
  27.7 0.0 copy-done.1
  27.7 0.0 copy-done.2
  27.7 0.0 copy-done.3
  27.7 0.0 copy-done.4
  27.7 0.0 copy-done.5
  27.7 2.1 %conditional.1 = (f32[36,32,256]{2,1,0:T(8,128)}) conditional(s32[]{:T(128)} %bitcast.8, (s32[8,128]{1,0:T(8,128)S(1)}, f32[32,128]{1,0:T(8,128)S(1)}, s16[128,8,128]{2,1,0:T(8,128)(2,1)S(1)}, f32[1152,256]{1,0:T(8,128)S(1)}) %tuple.13, (s32[16,1]{0,1:T(1,128)S(1)}, s32[16]{0:T(128)S(1)}, f32[1152,256]{1,0:T(8,128)S(1)}, f32[1152,256]{1,0:T(8,128)S(1)}, ...), branch_computations={%region_0.0_spmd, %region_1.0_spmd} | conditional | bytes 8 | solution.py:463
  27.7 2.1 %branch_0_fun.1 = f32[1152,256]{1,0:T(8,128)} custom-call(s32[8,128]{1,0:T(8,128)S(1)} %get-tuple-element.37.refs_0_, f32[32,128]{1,0:T(8,128)S(1)} %get-tuple-element.38.refs_1_, s16[128,8,128]{2,1,0:T(8,128)(2,1)S(1)} %get-tuple-element.39.refs_2_, f32[1152,256]{1,0:T(8,128)S(1)} %get-tuple-element.40.refs_3_), custom_call_target="tpu_custom_call" | custom-call | tf_op jit(solution)/shard_map/cond/branch_0_fun/pallas_call | solution.py:448
Async XLA Ops:
  0.0 27.7 %copy-start = (bf16[16,128,1024]{2,1,0:T(8,128)(2,1)S(1)}, bf16[16,128,1024]{2,1,0:T(8,128)(2,1)}, u32[]{:S(2)}) copy-start(bf16[16,128,1024]{2,1,0:T(8,128)(2,1)} %refs_4_.1) | copy-start | bytes 12582916
  0.0 27.7 %copy-start.1 = (f32[36,32,256]{2,1,0:T(8,128)S(1)}, f32[36,32,256]{2,1,0:T(8,128)}, u32[]{:S(2)}) copy-start(f32[36,32,256]{2,1,0:T(8,128)} %param.8) | copy-start | bytes 3538948
  0.0 27.7 %copy-start.2 = (f32[36,32,256]{2,1,0:T(8,128)S(1)}, f32[36,32,256]{2,1,0:T(8,128)}, u32[]{:S(2)}) copy-start(f32[36,32,256]{2,1,0:T(8,128)} %param.9) | copy-start | bytes 3538948
  0.0 27.7 %copy-start.3 = (bf16[16,128]{1,0:T(8,128)(2,1)S(1)}, bf16[16,128]{1,0:T(8,128)(2,1)}, u32[]{:S(2)}) copy-start(bf16[16,128]{1,0:T(8,128)(2,1)} %refs_5_.1) | copy-start | bytes 12292
  0.0 27.7 %copy-start.4 = (s32[16,1]{0,1:T(1,128)S(1)}, s32[16,1]{0,1:T(1,128)}, u32[]{:S(2)}) copy-start(s32[16,1]{0,1:T(1,128)} %param.11) | copy-start | bytes 196
  0.0 27.7 %copy-start.5 = (s32[16]{0:T(128)S(1)}, s32[16]{0:T(128)}, u32[]{:S(2)}) copy-start(s32[16]{0:T(128)} %param.12) | copy-start | bytes 196

commit v4 on v3

--- a/solution.py
+++ b/solution.py
@@ -8,9 +8,10 @@
 from jax.sharding import PartitionSpec as P
 
 CAP = 6
-MAIN = ((0, 1), (1, 4))
+MAIN = ((0, 1), (1, 2), (2, 4))
 REST = ((4, CAP),)
 LEVELS = 65535.0
+MARGIN = 1.01
 HALF = 32768
 LANES = 128
 SUBLANES = 8
@@ -39,10 +40,10 @@
     wide = high - low
     slab_hbm, block_hbm, image_hbm, sens_hbm, sys_hbm, bg_hbm, entry_ref, scale_ref, back_ref, ratio_ref, more_ref = refs[:11]
     (
-        turned_v, asked_ref, slab_v, block_v, bg_v, scale_v, image_v, sens_v, blocks_v, sys_v, mine_v, list_v, mine_s, list_s, asked_s, sums_v,
+        turned_v, asked_ref, slab_v, block_v, bg_v, scale_v, image_v, sens_v, blocks_v, sys_v, mine_v, list_v, mine_s, list_s, asked_s,
         local_sem, id_sem, scale_sem, fetch_sem, back_sem,
-    ) = refs[11:32]
-    per_part = [refs[32 + 4 * c:36 + 4 * c] for c in range(len(parts))]
+    ) = refs[11:31]
+    per_part = [refs[31 + 4 * c:35 + 4 * c] for c in range(len(parts))]
     me = lax.axis_index("slab") * reps + lax.axis_index("rep")
     lane_tiles = image_v.shape[1] // LANES
 
@@ -163,6 +164,31 @@
 
     groups = image_v.shape[0] // SUBLANES
     lax.fori_loop(0, groups, cut, 0, unroll=4)
+    load_bg.wait()
+    background = bg_v[...].astype(jnp.float32)
+    load_sys.wait()
+    most = (MARGIN / background).astype(jnp.bfloat16)
+    tops = []
+    for t in range(tiles):
+        bound = jnp.dot(most, sys_v[t], preferred_element_type=jnp.float32)[t:t + 1]
+        top = bound[:, 0:LANES]
+        for q in range(1, bound.shape[1] // LANES):
+            top = jnp.maximum(top, bound[:, q * LANES:(q + 1) * LANES])
+        tops.append(top)
+    peak = jnp.maximum(jnp.max(jnp.concatenate(tops, axis=0), axis=1, keepdims=True), 1e-33)
+    peaks = jnp.transpose(peak)
+    scale_v[...] = tabled(peaks * (1.0 / LEVELS), (low, high), jnp.zeros((n, LANES), jnp.float32))
+    scale_ref[pl.ds(0, 1), :] = scale_v[pl.ds(me, 1), :]
+
+    def give_scale(i):
+        d = me ^ i
+        pltpu.make_async_remote_copy(
+            src_ref=scale_v.at[pl.ds(d, 1)], dst_ref=scale_ref.at[pl.ds(i, 1)],
+            send_sem=scale_sem.at[0], recv_sem=scale_sem.at[1],
+            device_id=device(d), device_id_type=MESH,
+        ).start()
+
+    each_partner(give_scale)
     load_sens.wait()
 
     def divide(g, c):
@@ -171,17 +197,16 @@
         return c
 
     lax.fori_loop(0, groups, divide, 0, unroll=4)
-    load_bg.wait()
-    background = bg_v[...]
-    columns = []
+    columns, gains = [], []
     for pick in hots:
         if pick is None:
-            columns.append(jnp.transpose(background.astype(jnp.float32)))
+            columns.append(jnp.transpose(background))
+            gains.append(LEVELS / peak)
         else:
             ones = jnp.where(pick, 1.0, 0.0)
-            chosen = jnp.dot(ones.astype(jnp.bfloat16), background, preferred_element_type=jnp.float32)
+            chosen = jnp.dot(ones.astype(jnp.bfloat16), bg_v[...], preferred_element_type=jnp.float32)
             columns.append(jnp.transpose(chosen + (1.0 - jnp.sum(ones, axis=1, keepdims=True))))
-    load_sys.wait()
+            gains.append(jnp.sum(jnp.where(pick, LEVELS / peaks, 0.0), axis=1, keepdims=True))
     rest = asked_ref.at[pl.ds(1, n - 1)]
     pltpu.make_async_copy(rest, rest, id_sem.at[1]).wait()
     turned_v[:, 0:n] = jnp.transpose(asked_ref[...])[0:SUBLANES]
@@ -237,7 +262,6 @@
 
     pieces = block_rows * lane_tiles
     places = [(p % block_rows) * lane_tiles + p // block_rows for p in range(pieces)]
-    scales = jnp.zeros((n, LANES), jnp.float32)
     for c, (lo, hi) in enumerate(parts):
         span, (send_f, recv_f, bp_v, send_b) = hi - lo, per_part[c]
         others = recv_f.at[pl.ds(span, (n - 1) * span)]
@@ -259,16 +283,10 @@
                 total = term if total is None else total + term
             forward = jnp.where(column == j, jnp.sum(total, axis=1, keepdims=True), forward)
         inverse = jnp.transpose(1.0 / (forward + columns[c])).astype(jnp.bfloat16)
-        tops = []
         for j in range(count):
             back = jnp.dot(inverse, sys_v[chosen[j]], preferred_element_type=jnp.float32)
             tile = jnp.concatenate([back[j:j + 1, q * LANES:(q + 1) * LANES] for q in places], axis=0)
-            sums_v[j] = tile
-            tops.append(jnp.max(tile, axis=0, keepdims=True))
-        peak = jnp.maximum(jnp.max(jnp.concatenate(tops, axis=0), axis=1, keepdims=True), 1e-33)
-        gain = LEVELS / peak
-        for j in range(count):
-            level = jnp.round(sums_v[j] * gain[j:j + 1, :]).astype(jnp.int32) - HALF
+            level = jnp.round(tile * gains[c][j:j + 1, :]).astype(jnp.int32) - HALF
             bp_v[j] = jnp.clip(level, -HALF, HALF - 1).astype(jnp.int16)
 
         def routed(d, k):
@@ -287,24 +305,6 @@
         each_partner(give)
         for k in range(span):
             back_ref[(lo - low) * n + k] = routed(me, k)
-        if pick is None:
-            peaks = jnp.transpose(peak)
-        else:
-            peaks = jnp.sum(jnp.where(pick[:count], peak, 0.0), axis=0, keepdims=True)
-        scales = tabled(peaks * (1.0 / LEVELS), (lo, hi), scales)
-
-    scale_v[...] = scales
-    scale_ref[pl.ds(0, 1), :] = scale_v[pl.ds(me, 1), :]
-
-    def give_scale(i):
-        d = me ^ i
-        pltpu.make_async_remote_copy(
-            src_ref=scale_v.at[pl.ds(d, 1)], dst_ref=scale_ref.at[pl.ds(i, 1)],
-            send_sem=scale_sem.at[0], recv_sem=scale_sem.at[1],
-            device_id=device(d), device_id_type=MESH,
-        ).start()
-
-    each_partner(give_scale)
     scaled = scale_ref.at[pl.ds(1, n - 1)]
     pltpu.make_async_copy(scaled, scaled, scale_sem.at[0]).wait()
     pltpu.make_async_copy(rest, rest, id_sem.at[0]).wait()
@@ -421,7 +421,6 @@
                 pltpu.SMEM((n, LANES), jnp.int32),
                 pltpu.SMEM((rows_of_lists, LANES), jnp.int32),
                 pltpu.SMEM((SUBLANES, max(n, LANES)), jnp.int32),
-                pltpu.VMEM((tiles, sub, LANES), jnp.float32),
                 pltpu.SemaphoreType.DMA((7,)),
                 pltpu.SemaphoreType.DMA((2,)),
                 pltpu.SemaphoreType.DMA((2,)),

time: 29.8 us -> 29 us (0.973)
  Pallas kernels: 29.7 us -> 28.7 us
    pallas_call x1, Pallas kernels: 27.6 us -> 26.6 us  [exchange(): pl.pallas_call(functools.partial(exchange_kernel, (n, reps, tiles, block_...]
where the time goes in v4:
time: 29 us; the launch traced here: 28.8 us
  Pallas kernels  28.7 us (99%)
    pallas_call x1, Pallas kernels, exchange(): pl.pallas_call(functools.partial(exchange_kernel, (n, reps, tiles, block_...  26.6 us
    pallas_call x1, Pallas kernels, update(): pl.pallas_call(functools.partial(update_kernel, (block_rows,), widths), o...  2.06 us

profile of v4, /device:TPU:0, one launch (start us, length us, event | category | flops | bytes accessed | tf_op | source)
XLA Modules:
  0.0 28.8 jit_solution(11732667013151293813)
XLA Ops:
  0.0 0.0 copy-start
  0.0 0.0 copy-start.1
  0.0 0.0 copy-start.2
  0.0 0.0 copy-start.3
  0.0 0.0 copy-start.4
  0.0 0.0 copy-start.5
  0.0 26.6 %shard_map.66 = (s32[8,128]{1,0:T(8,128)S(1)}, f32[32,128]{1,0:T(8,128)S(1)}, s16[128,8,128]{2,1,0:T(8,128)(2,1)S(1)}, f32[1152,256]{1,0:T(8,128)S(1)}, s32[1,128]{1,0:T(1,128)S(1)}) custom-call(s32[1,16]{1,0:T(1,128)} %bitcast.17, s32[1,16]{1,0:T(1,128)} %bitcast.19, f32[1152,256]{1,0:T(8,128)} %bitcast.11, f32[1152,256]{1,0:T(8,128)} %bitcast.13, ...), custom_call_target="tpu_custom_call" | custom-call | tf_op jit(solution)/shard_map/pallas_call | solution.py:397
  26.7 0.0 copy-done
  26.7 0.0 copy-done.1
  26.7 0.0 copy-done.2
  26.7 0.0 copy-done.3
  26.7 0.0 copy-done.4
  26.8 0.0 copy-done.5
  26.8 2.1 %conditional.1 = (f32[36,32,256]{2,1,0:T(8,128)}) conditional(s32[]{:T(128)} %bitcast.8, (s32[8,128]{1,0:T(8,128)S(1)}, f32[32,128]{1,0:T(8,128)S(1)}, s16[128,8,128]{2,1,0:T(8,128)(2,1)S(1)}, f32[1152,256]{1,0:T(8,128)S(1)}) %tuple.13, (s32[16,1]{0,1:T(1,128)S(1)}, s32[16]{0:T(128)S(1)}, f32[1152,256]{1,0:T(8,128)S(1)}, f32[1152,256]{1,0:T(8,128)S(1)}, ...), branch_computations={%region_0.0_spmd, %region_1.0_spmd} | conditional | bytes 8 | solution.py:462
  26.8 2.1 %branch_0_fun.1 = f32[1152,256]{1,0:T(8,128)} custom-call(s32[8,128]{1,0:T(8,128)S(1)} %get-tuple-element.37.refs_0_, f32[32,128]{1,0:T(8,128)S(1)} %get-tuple-element.38.refs_1_, s16[128,8,128]{2,1,0:T(8,128)(2,1)S(1)} %get-tuple-element.39.refs_2_, f32[1152,256]{1,0:T(8,128)S(1)} %get-tuple-element.40.refs_3_), custom_call_target="tpu_custom_call" | custom-call | tf_op jit(solution)/shard_map/cond/branch_0_fun/pallas_call | solution.py:447
Async XLA Ops:
  0.0 26.7 %copy-start = (bf16[16,128,1024]{2,1,0:T(8,128)(2,1)S(1)}, bf16[16,128,1024]{2,1,0:T(8,128)(2,1)}, u32[]{:S(2)}) copy-start(bf16[16,128,1024]{2,1,0:T(8,128)(2,1)} %refs_4_.1) | copy-start | bytes 12582916
  0.0 26.7 %copy-start.1 = (f32[36,32,256]{2,1,0:T(8,128)S(1)}, f32[36,32,256]{2,1,0:T(8,128)}, u32[]{:S(2)}) copy-start(f32[36,32,256]{2,1,0:T(8,128)} %param.8) | copy-start | bytes 3538948
  0.0 26.7 %copy-start.2 = (f32[36,32,256]{2,1,0:T(8,128)S(1)}, f32[36,32,256]{2,1,0:T(8,128)}, u32[]{:S(2)}) copy-start(f32[36,32,256]{2,1,0:T(8,128)} %param.9) | copy-start | bytes 3538948
  0.0 26.7 %copy-start.3 = (bf16[16,128]{1,0:T(8,128)(2,1)S(1)}, bf16[16,128]{1,0:T(8,128)(2,1)}, u32[]{:S(2)}) copy-start(bf16[16,128]{1,0:T(8,128)(2,1)} %refs_5_.1) | copy-start | bytes 12292
  0.0 26.7 %copy-start.4 = (s32[16,1]{0,1:T(1,128)S(1)}, s32[16,1]{0,1:T(1,128)}, u32[]{:S(2)}) copy-start(s32[16,1]{0,1:T(1,128)} %param.11) | copy-start | bytes 196
  0.0 26.7 %copy-start.5 = (s32[16]{0:T(128)S(1)}, s32[16]{0:T(128)}, u32[]{:S(2)}) copy-start(s32[16]{0:T(128)} %param.12) | copy-start | bytes 196

commit v5 on v4

--- a/solution.py
+++ b/solution.py
@@ -12,6 +12,7 @@
 REST = ((4, CAP),)
 LEVELS = 65535.0
 MARGIN = 1.01
+STORES = 4
 HALF = 32768
 LANES = 128
 SUBLANES = 8
@@ -38,12 +39,12 @@
     n, reps, tiles, block_rows, per_owner = sizes
     low, high = parts[0][0], parts[-1][1]
     wide = high - low
-    slab_hbm, block_hbm, image_hbm, sens_hbm, sys_hbm, bg_hbm, entry_ref, scale_ref, back_ref, ratio_ref, more_ref = refs[:11]
+    slab_hbm, block_hbm, image_hbm, sens_hbm, sys_hbm, bg_hbm, entry_s, factor_s, back_ref, ratio_ref, more_ref = refs[:11]
     (
-        turned_v, asked_ref, slab_v, block_v, bg_v, scale_v, image_v, sens_v, blocks_v, sys_v, mine_v, list_v, mine_s, list_s, asked_s,
+        turned_v, entry_ref, factor_ref, scale_ref, asked_ref, slab_v, block_v, bg_v, scale_v, image_v, sens_v, blocks_v, sys_v, mine_v, list_v, mine_s, list_s, asked_s,
         local_sem, id_sem, scale_sem, fetch_sem, back_sem,
-    ) = refs[11:31]
-    per_part = [refs[31 + 4 * c:35 + 4 * c] for c in range(len(parts))]
+    ) = refs[11:34]
+    per_part = [refs[34 + 4 * c:38 + 4 * c] for c in range(len(parts))]
     me = lax.axis_index("slab") * reps + lax.axis_index("rep")
     lane_tiles = image_v.shape[1] // LANES
 
@@ -247,18 +248,34 @@
     room = entry_ref.shape[1]
     position = lax.broadcasted_iota(jnp.int32, (n, room), 1)
     filled = jnp.zeros((1, 1), jnp.int32)
-    entries = [jnp.zeros((1, room), jnp.int32) for _ in range(3)]
+    entries = [jnp.zeros((1, room), jnp.int32) for _ in range(2)]
     for lo, hi in parts:
         for k in range(lo - low, hi - low):
             value_k = asked[:, k:k + 1]
             mine_k = (position == ahead[:, k:k + 1] + filled) & (value_k > 0)
             row_k = (lo - low) * n + source * (hi - lo) + k - (lo - low)
-            facts = (row_k, split(value_k - 1, tiles)[0], source * wide + k)
+            facts = (row_k, split(value_k - 1, tiles)[0])
             for f, fact in enumerate(facts):
                 entries[f] += jnp.sum(jnp.where(mine_k, fact, 0), axis=0, keepdims=True)
             filled += jnp.sum(jnp.where(value_k > 0, 1, 0), axis=0, keepdims=True)
+    scaled = scale_ref.at[pl.ds(1, n - 1)]
+    pltpu.make_async_copy(scaled, scaled, scale_sem.at[1]).wait()
+    factor = jnp.zeros((1, room), jnp.float32)
+    filled_by = jnp.zeros((1, 1), jnp.int32)
+    for k in range(wide):
+        value_k = asked[:, k:k + 1]
+        mine_k = (position == ahead[:, k:k + 1] + filled_by) & (value_k > 0)
+        factor += jnp.sum(jnp.where(mine_k, scale_ref[:, k:k + 1], 0.0), axis=0, keepdims=True)
+        filled_by += jnp.sum(jnp.where(value_k > 0, 1, 0), axis=0, keepdims=True)
+    factor_ref[0:1, :] = factor
     for f, fact in enumerate(entries + [jnp.broadcast_to(filled, (1, room))]):
         entry_ref[f:f + 1, :] = fact
+    keep = [
+        pltpu.make_async_copy(entry_ref, entry_s, local_sem.at[2]),
+        pltpu.make_async_copy(factor_ref, factor_s, local_sem.at[3]),
+    ]
+    for copy in keep:
+        copy.start()
 
     pieces = block_rows * lane_tiles
     places = [(p % block_rows) * lane_tiles + p // block_rows for p in range(pieces)]
@@ -305,7 +322,8 @@
         each_partner(give)
         for k in range(span):
             back_ref[(lo - low) * n + k] = routed(me, k)
-    scaled = scale_ref.at[pl.ds(1, n - 1)]
+    for copy in keep:
+        copy.wait()
     pltpu.make_async_copy(scaled, scaled, scale_sem.at[0]).wait()
     pltpu.make_async_copy(rest, rest, id_sem.at[0]).wait()
     for c, (lo, hi) in enumerate(parts):
@@ -316,24 +334,12 @@
         pltpu.make_async_copy(given, given, back_sem.at[2 * c]).wait()
         landed = back_ref.at[pl.ds((lo - low) * n + span, (n - 1) * span)]
         pltpu.make_async_copy(landed, landed, back_sem.at[2 * c + 1]).wait()
-    pltpu.make_async_copy(scaled, scaled, scale_sem.at[1]).wait()
-
-
-def update_kernel(sizes, widths, *refs):
-    block_rows, = sizes
-    tables = 3 * len(widths)
+
+
+def update_kernel(block_rows, copies, *refs):
+    tables = 3 * copies
     ratio_ref, out_hbm = refs[tables:tables + 2]
-    out_ref, in_sem, out_sem = refs[-3:]
-    staged = refs[tables + 2:-3]
-    loads = []
-    for j in range(len(widths)):
-        entry_s, scale_s, turned_v = staged[3 * j:3 * j + 3]
-        loads.append(pltpu.make_async_copy(refs[3 * j], entry_s, in_sem.at[2 * j]))
-        loads[-1].start()
-        scale_ref = refs[3 * j + 1]
-        turned_v[:, 0:scale_ref.shape[0]] = jnp.transpose(scale_ref[...])[0:SUBLANES]
-        loads.append(pltpu.make_async_copy(turned_v, scale_s, in_sem.at[2 * j + 1]))
-        loads[-1].start()
+    out_ref, out_sem = refs[-2:]
     lane_tiles = out_ref.shape[1] // LANES
     per_group = SUBLANES // block_rows
     groups = out_ref.shape[0] // SUBLANES
@@ -343,17 +349,14 @@
         return c
 
     lax.fori_loop(0, groups, clear, 0, unroll=8)
-    for load in loads:
-        load.wait()
     part_of_row = split(lax.broadcasted_iota(jnp.int32, (SUBLANES, LANES), 0), block_rows)[0]
-    for j, wide in enumerate(widths):
-        entry_s, scale_s, back_ref = staged[3 * j], staged[3 * j + 1], refs[3 * j + 2]
+    for j in range(copies):
+        entry_s, factor_s, back_ref = refs[3 * j:3 * j + 3]
 
         def one(e, c):
-            row, block, source = entry_s[0, e], entry_s[1, e], entry_s[2, e]
-            i, k = split(source, wide)
+            row, block = entry_s[0, e], entry_s[1, e]
             g, part = split(block, per_group)
-            level = (back_ref[row].astype(jnp.int32) + HALF).astype(jnp.float32) * scale_s[k, i]
+            level = (back_ref[row].astype(jnp.int32) + HALF).astype(jnp.float32) * factor_s[0, e]
             rows = pl.ds(pl.multiple_of(g * SUBLANES, SUBLANES), SUBLANES)
             for h in range(lane_tiles):
                 cols = slice(h * LANES, (h + 1) * LANES)
@@ -361,10 +364,15 @@
                 out_ref[rows, cols] += jnp.where(part_of_row == part, piece * ratio_ref[rows, cols], 0.0)
             return c
 
-        lax.fori_loop(0, entry_s[3, 0], one, 0)
-    store = pltpu.make_async_copy(out_ref, out_hbm, out_sem)
-    store.start()
-    store.wait()
+        lax.fori_loop(0, entry_s[2, 0], one, 0)
+    stores = []
+    for c in range(STORES):
+        first, last = groups * c // STORES * SUBLANES, groups * (c + 1) // STORES * SUBLANES
+        span = pl.ds(first, last - first)
+        stores.append(pltpu.make_async_copy(out_ref.at[span], out_hbm.at[span], out_sem.at[c]))
+        stores[-1].start()
+    for store in stores:
+        store.wait()
 
 
 def local(image, sensitivity, system_blocks, tile_slab, tile_block, background):
@@ -381,9 +389,11 @@
 
     hbm = pl.BlockSpec(memory_space=pltpu.HBM)
     vmem = pl.BlockSpec(memory_space=pltpu.VMEM)
+    smem = pl.BlockSpec(memory_space=pltpu.SMEM)
 
     def exchange(parts, collective_id):
         wide = parts[-1][1] - parts[0][0]
+        room_of_entries = -(-n * wide // LANES) * LANES
         rows_of_lists = 3 * SUBLANES * len(parts)
         buffers = []
         for lo, hi in parts:
@@ -397,16 +407,19 @@
         return pl.pallas_call(
             functools.partial(exchange_kernel, (n, reps, tiles, block_rows, per_owner), parts),
             out_shape=(
-                pltpu.VMEM((SUBLANES, -(-n * wide // LANES) * LANES), jnp.int32),
-                pltpu.VMEM((n, LANES), jnp.float32),
+                pltpu.SMEM((SUBLANES, room_of_entries), jnp.int32),
+                pltpu.SMEM((SUBLANES, room_of_entries), jnp.float32),
                 pltpu.VMEM((n * wide, sub, LANES), jnp.int16),
                 pltpu.VMEM(image2.shape, jnp.float32),
                 pltpu.VMEM((1, LANES), jnp.int32),
             ),
             in_specs=[hbm] * 6,
-            out_specs=(vmem,) * 5,
+            out_specs=(smem,) * 2 + (vmem,) * 3,
             scratch_shapes=[
                 pltpu.VMEM((SUBLANES, max(n, LANES)), jnp.int32),
+                pltpu.VMEM((SUBLANES, room_of_entries), jnp.int32),
+                pltpu.VMEM((SUBLANES, room_of_entries), jnp.float32),
+                pltpu.VMEM((n, LANES), jnp.float32),
                 pltpu.VMEM((n, LANES), jnp.int32),
                 pltpu.VMEM((1, tiles), jnp.int32),
                 pltpu.VMEM((1, tiles), jnp.int32),
@@ -435,25 +448,14 @@
 
     def update(*results):
         tables = [table for result in results for table in result[:3]]
-        widths = tuple(result[2].shape[0] // n for result in results)
-        staged = []
-        for entries, _, _ in (result[:3] for result in results):
-            turned = (SUBLANES, max(n, LANES))
-            staged += [
-                pltpu.SMEM(entries.shape, jnp.int32),
-                pltpu.SMEM(turned, jnp.float32),
-                pltpu.VMEM(turned, jnp.float32),
-            ]
         return pl.pallas_call(
-            functools.partial(update_kernel, (block_rows,), widths),
+            functools.partial(update_kernel, block_rows, len(results)),
             out_shape=pltpu.HBM(image2.shape, jnp.float32),
-            in_specs=[vmem] * (len(tables) + 1),
+            in_specs=[smem, smem, vmem] * len(results) + [vmem],
             out_specs=hbm,
             scratch_shapes=[
-                *staged,
                 pltpu.VMEM(image2.shape, jnp.float32),
-                pltpu.SemaphoreType.DMA((2 * len(results),)),
-                pltpu.SemaphoreType.DMA,
+                pltpu.SemaphoreType.DMA((STORES,)),
             ],
             compiler_params=pltpu.CompilerParams(vmem_limit_bytes=VMEM_LIMIT),
         )(*tables, results[0][3])

time: 29 us -> 28.4 us (0.979)
  Pallas kernels: 28.7 us -> 28.1 us
    pallas_call x1, Pallas kernels: 2.06 us -> 1.53 us  [update(): pl.pallas_call(functools.partial(update_kernel, block_rows, len(results))...]
where the time goes in v5:
time: 28.4 us; the launch traced here: 28.3 us
  Pallas kernels  28.1 us (99%)
    pallas_call x1, Pallas kernels, exchange(): pl.pallas_call(functools.partial(exchange_kernel, (n, reps, tiles, block_...  26.6 us
    pallas_call x1, Pallas kernels, update(): pl.pallas_call(functools.partial(update_kernel, block_rows, len(results))...  1.53 us

profile of v5, /device:TPU:0, one launch (start us, length us, event | category | flops | bytes accessed | tf_op | source)
XLA Modules:
  0.0 28.3 jit_solution(18017904539352057616)
XLA Ops:
  0.0 0.0 copy-start
  0.0 0.0 copy-start.1
  0.0 0.0 copy-start.2
  0.0 0.0 copy-start.3
  0.0 0.0 copy-start.4
  0.0 0.0 copy-start.5
  0.0 26.6 %shard_map.66 = (s32[8,128]{1,0:T(8,128)S(4)}, f32[8,128]{1,0:T(8,128)S(4)}, s16[128,8,128]{2,1,0:T(8,128)(2,1)S(1)}, f32[1152,256]{1,0:T(8,128)S(1)}, s32[1,128]{1,0:T(1,128)S(1)}) custom-call(s32[1,16]{1,0:T(1,128)} %bitcast.17, s32[1,16]{1,0:T(1,128)} %bitcast.19, f32[1152,256]{1,0:T(8,128)} %bitcast.11, f32[1152,256]{1,0:T(8,128)} %bitcast.13, ...), custom_call_target="tpu_custom_call" | custom-call | tf_op jit(solution)/shard_map/pallas_call | solution.py:407
  26.7 0.0 copy-done
  26.7 0.0 copy-done.1
  26.7 0.0 copy-done.2
  26.7 0.0 copy-done.3
  26.7 0.0 copy-done.4
  26.7 0.0 copy-done.5
  26.7 1.5 %conditional.1 = (f32[36,32,256]{2,1,0:T(8,128)}) conditional(s32[]{:T(128)} %bitcast.8, (s32[8,128]{1,0:T(8,128)S(4)}, f32[8,128]{1,0:T(8,128)S(4)}, s16[128,8,128]{2,1,0:T(8,128)(2,1)S(1)}, f32[1152,256]{1,0:T(8,128)S(1)}) %tuple.13, (s32[16,1]{0,1:T(1,128)S(1)}, s32[16]{0:T(128)S(1)}, f32[1152,256]{1,0:T(8,128)S(1)}, f32[1152,256]{1,0:T(8,128)S(1)}, ...), branch_computations={%region_0.0_spmd, %region_1.0_spmd} | conditional | bytes 8 | solution.py:464
  26.7 1.5 %branch_0_fun.1 = f32[1152,256]{1,0:T(8,128)} custom-call(s32[8,128]{1,0:T(8,128)S(4)} %get-tuple-element.37.refs_0_, f32[8,128]{1,0:T(8,128)S(4)} %get-tuple-element.38.refs_1_, s16[128,8,128]{2,1,0:T(8,128)(2,1)S(1)} %get-tuple-element.39.refs_2_, f32[1152,256]{1,0:T(8,128)S(1)} %get-tuple-element.40.refs_3_), custom_call_target="tpu_custom_call" | custom-call | tf_op jit(solution)/shard_map/cond/branch_0_fun/pallas_call | solution.py:451
Async XLA Ops:
  0.0 26.7 %copy-start = (bf16[16,128,1024]{2,1,0:T(8,128)(2,1)S(1)}, bf16[16,128,1024]{2,1,0:T(8,128)(2,1)}, u32[]{:S(2)}) copy-start(bf16[16,128,1024]{2,1,0:T(8,128)(2,1)} %refs_4_.1) | copy-start | bytes 12582916
  0.0 26.7 %copy-start.1 = (f32[36,32,256]{2,1,0:T(8,128)S(1)}, f32[36,32,256]{2,1,0:T(8,128)}, u32[]{:S(2)}) copy-start(f32[36,32,256]{2,1,0:T(8,128)} %param.8) | copy-start | bytes 3538948
  0.0 26.7 %copy-start.2 = (f32[36,32,256]{2,1,0:T(8,128)S(1)}, f32[36,32,256]{2,1,0:T(8,128)}, u32[]{:S(2)}) copy-start(f32[36,32,256]{2,1,0:T(8,128)} %param.9) | copy-start | bytes 3538948
  0.0 26.7 %copy-start.3 = (bf16[16,128]{1,0:T(8,128)(2,1)S(1)}, bf16[16,128]{1,0:T(8,128)(2,1)}, u32[]{:S(2)}) copy-start(bf16[16,128]{1,0:T(8,128)(2,1)} %refs_5_.1) | copy-start | bytes 12292
  0.0 26.7 %copy-start.4 = (s32[16,1]{0,1:T(1,128)S(1)}, s32[16,1]{0,1:T(1,128)}, u32[]{:S(2)}) copy-start(s32[16,1]{0,1:T(1,128)} %param.11) | copy-start | bytes 196
  0.0 26.7 %copy-start.5 = (s32[16]{0:T(128)S(1)}, s32[16]{0:T(128)}, u32[]{:S(2)}) copy-start(s32[16]{0:T(128)} %param.12) | copy-start | bytes 196
